TPU v7x, 256 devices: a whole 4x4x8 slice. The times are simulated.
256 devices in a mesh: space: 32 (over z, y_hi, core), tm: 8 (over x, y_lo).
Axes of the slice: x: 4, y: 4 (y_hi: 2, y_lo: 2; y = y_hi * 2 + y_lo), z: 8, core: 2. Of those that a mesh axis runs over, the one named last changes fastest.
Arguments:
- solutions: bfloat16 [8, 12, 16384, 128], P('tm', None, 'space'), may hold values from -6 to 6
- noise: int32 [8, 64, 12, 16384], P('tm', None, None, 'space'), may hold values from 0 to 3
- momenta: int32 [27, 3], replicated, may hold values from -2 to 2
- pairs: int32 [64, 2], P('tm'), may hold values from 0 to 7
Outputs:
- mesons: float32 [8, 2, 27, 64, 64], P('tm', None, None, 'space')
- correlators: float32 [64, 2, 27], P('tm')
All inputs are finite; a program needn't handle non-finite values.
Results may differ from a plain program's by a relative error of at most 0.002.
Values sent between devices are 32-bit elements; how exact they have to be, the bound alone decides.
A program may use at most 64 MiB of HBM per device.

v0:
```python
import math

import jax
import jax.numpy as jnp
from jax import lax
from jax.sharding import PartitionSpec as P

EXTENT = 48


def in_blocks(array, dim, length):
    before, after = (array.shape[:dim], array.shape[dim + 1 :])
    return jnp.moveaxis(array.reshape(*before, length, -1, *after), dim, 0)


def summed_on_arrival(array, axis, dim):
    pieces = in_blocks(array, dim, lax.axis_size(axis))
    arrived = lax.all_to_all(pieces, axis, split_axis=0, concat_axis=0, tiled=True)
    return arrived.sum(axis=0)


def copy_for_each(array, axis):
    copies = jnp.broadcast_to(array, (lax.axis_size(axis), *array.shape))
    return lax.all_to_all(copies, axis, split_axis=0, concat_axis=0, tiled=True)


def laid_out(pieces, dim):
    pieces = jnp.moveaxis(pieces, 0, dim)
    dims = pieces.shape
    return pieces.reshape(*dims[:dim], dims[dim] * dims[dim + 1], *dims[dim + 2 :])


def gathered_copies(array, axis, dim):
    pieces = copy_for_each(array, axis)
    return laid_out(pieces, dim)


def over_copies(array, axis):
    return copy_for_each(array, axis).sum(axis=0)


def phase_weights(noise_block, momenta, coords):
    qdotx = (
        momenta[:, 0:1] * coords[0][None, :]
        + momenta[:, 1:2] * coords[1][None, :]
        + momenta[:, 2:3] * coords[2][None, :]
    )
    base_index = qdotx % EXTENT
    angle = base_index.astype(jnp.float32) * jnp.float32(2.0 * math.pi / EXTENT)
    base_re = jnp.cos(angle).astype(jnp.bfloat16)[:, None, None, :]
    base_im = (-jnp.sin(angle)).astype(jnp.bfloat16)[:, None, None, :]
    turns = (noise_block % 4)[None, :, :, :]
    weight_re = jnp.where(
        turns == 0,
        base_re,
        jnp.where(turns == 1, base_im, jnp.where(turns == 2, -base_re, -base_im)),
    )
    weight_im = jnp.where(
        turns == 0,
        base_im,
        jnp.where(turns == 1, -base_re, jnp.where(turns == 2, -base_im, base_re)),
    )
    rows = momenta.shape[0] * noise_block.shape[0]
    cols = noise_block.shape[1] * noise_block.shape[2]
    return (weight_re.reshape(rows, cols), weight_im.reshape(rows, cols))


def partial_field(vectors, sources, momenta, offset):
    spincol, sites, width = vectors.shape
    nvec = width // 2
    moms = momenta.shape[0]
    block = min(128, sites)
    nblocks = sites // block

    def one_block(step, total):
        first = (step * block).astype(jnp.int32)
        noise_block = lax.dynamic_slice_in_dim(sources, first, block, 2)
        vec_block = lax.dynamic_slice_in_dim(vectors, first, block, 1)
        glob = offset + first + jnp.arange(block, dtype=jnp.int32)
        coords = (glob % EXTENT, glob // EXTENT % EXTENT, glob // (EXTENT * EXTENT))
        weight_re, weight_im = phase_weights(noise_block, momenta, coords)
        stacked = vec_block.reshape(spincol * block, width)
        left = jnp.dot(weight_re, stacked, preferred_element_type=jnp.float32)
        right = jnp.dot(weight_im, stacked, preferred_element_type=jnp.float32)
        real_part = left[:, :nvec] - right[:, nvec:]
        imag_part = left[:, nvec:] + right[:, :nvec]
        return total + jnp.stack([real_part, imag_part], 0)

    start = jnp.zeros((2, moms * nvec, nvec), jnp.float32)
    total = lax.fori_loop(0, nblocks, one_block, start)
    return total.reshape(2, moms, nvec, nvec)


def pair_traces(fields, pairs):
    nslices = fields.shape[0]
    slots = jnp.arange(nslices, dtype=jnp.int32)
    pick_sink = (pairs[:, 1][:, None] == slots[None, :]).astype(jnp.float32)
    pick_source = (pairs[:, 0][:, None] == slots[None, :]).astype(jnp.float32)
    sink = jnp.einsum("kt,tcpij->kcpij", pick_sink, fields, precision=lax.Precision.HIGHEST)
    source = jnp.einsum("kt,tcpij->kcpij", pick_source, fields, precision=lax.Precision.HIGHEST)
    real_part = jnp.sum(sink[:, 0] * source[:, 0] + sink[:, 1] * source[:, 1], axis=(2, 3))
    imag_part = jnp.sum(sink[:, 1] * source[:, 0] - sink[:, 0] * source[:, 1], axis=(2, 3))
    return jnp.stack([real_part, imag_part], 1)


def local(solutions, noise, momenta, pairs):
    slice_count, spincol, sites_local, width = solutions.shape
    nvec = width // 2
    nspace = lax.axis_size("space")
    scale = 1.0 / math.sqrt(spincol * sites_local * nspace)
    offset = lax.axis_index("space") * sites_local
    terms = jnp.stack([partial_field(solutions[0], noise[0], momenta, offset) * scale], 0)
    mesons = summed_on_arrival(terms, "space", 3)
    every_slice = gathered_copies(mesons, "tm", 0)
    partial_traces = pair_traces(every_slice, pairs)
    correlators = over_copies(partial_traces, "space") / nvec
    return (mesons, correlators)


def solution(mesh):
    in_specs = (P("tm", None, "space", None), P("tm", None, None, "space"), P(), P("tm", None))
    out_specs = (P("tm", None, None, "space", None), P("tm", None, None))
    return jax.shard_map(local, mesh=mesh, in_specs=in_specs, out_specs=out_specs, check_vma=False)
```

profile of v0, /device:TPU:1, one launch (start us, length us, event | category | flops | bytes accessed | tf_op | source)
XLA Modules:
  0.0 147.4 jit_solution(9370178631061712609)
XLA Ops:
  0.7 3.8 %copy.60 = s32[1,64,12,512]{3,2,1,0:T(8,128)} copy(s32[1,64,12,512]{3,1,2,0:T(8,128)} %param.7) | data formatting | bytes 3145728 | tf_op args[1]
  4.4 64.5 %while.17 = (s32[]{:T(128)}, f32[2,1728,64]{2,1,0:T(8,128)S(1)}, s32[64,12,512]{2,1,0:T(8,128)}, s32[27,3]{0,1:T(4,128)S(1)}, s32[]{:T(128)}, /*index=5*/bf16[12...) while((s32[]{:T(128)}, f32[2,1728,64]{2,1,0:T(8,128)S(1)}, ...), condition=%wide.region_1.2_spmd.clone, body=%wide.region_0.1_spmd.clone.sunk | while | flops 1377275648 | bytes 30928840 | solution.py:90
  4.8 1.4 broadcast_compare_fusion.4
  6.3 5.9 %select_select_fusion.3 = (bf16[27,64,12,128]{3,2,1,0:T(8,128)(2,1)}, bf16[27,64,12,128]{3,2,1,0:T(8,128)(2,1)S(1)}) fusion(pred[64,12,128]{2,1,0:T(8,128)(4,1)S(1)} %get-tuple-element.305, pred[64,12,128]{2,1,0:T(8,128)(4,1)S(1)} %get-tuple-element.306, pred[64,12,128]{2,1,0:T(8,128)(4,1)S(1)} %get-tuple-element.307, ...), kind=kLoop, calls=%fused_computation.1.clone.1 | loop fusion | flops 15925248 | bytes 10939392 | tf_op jit(solution)/shard_map/while/body/eval_jaxpr/jit(_where)/select_n | solution.py:53
  13.2 4.6 %fusion.46 = f32[1728,128]{1,0:T(8,128)S(1)} fusion(bf16[1536,128]{1,0:T(8,128)(2,1)S(1)} %bitcast.77, bf16[216,8,12,128]{3,2,1,0:T(8,128)(2,1)} %bitcast.75), kind=kOutput, calls=%fused_computation.5.clone.1 | convolution fusion | flops 679477248 | bytes 6586368 | tf_op jit(solution)/shard_map/while/body/eval_jaxpr/dot_general | solution.py:83
  17.8 1.6 %fusion.45 = f32[1728,128]{1,0:T(8,128)S(1)} fusion(bf16[1536,128]{1,0:T(8,128)(2,1)S(1)} %bitcast.78, bf16[216,8,12,128]{3,2,1,0:T(8,128)(2,1)S(1)} %bitcast.74), kind=kOutput, calls=%fused_computation.2.clone.1 | convolution fusion | flops 679477248 | bytes 6586368 | tf_op jit(solution)/shard_map/while/body/eval_jaxpr/dot_general | solution.py:84
  20.9 1.4 broadcast_compare_fusion.4
  22.4 5.9 %select_select_fusion.3 = (bf16[27,64,12,128]{3,2,1,0:T(8,128)(2,1)}, bf16[27,64,12,128]{3,2,1,0:T(8,128)(2,1)S(1)}) fusion(pred[64,12,128]{2,1,0:T(8,128)(4,1)S(1)} %get-tuple-element.305, pred[64,12,128]{2,1,0:T(8,128)(4,1)S(1)} %get-tuple-element.306, pred[64,12,128]{2,1,0:T(8,128)(4,1)S(1)} %get-tuple-element.307, ...), kind=kLoop, calls=%fused_computation.1.clone.1 | loop fusion | flops 15925248 | bytes 10939392 | tf_op jit(solution)/shard_map/while/body/eval_jaxpr/jit(_where)/select_n | solution.py:53
  29.4 4.6 %fusion.46 = f32[1728,128]{1,0:T(8,128)S(1)} fusion(bf16[1536,128]{1,0:T(8,128)(2,1)S(1)} %bitcast.77, bf16[216,8,12,128]{3,2,1,0:T(8,128)(2,1)} %bitcast.75), kind=kOutput, calls=%fused_computation.5.clone.1 | convolution fusion | flops 679477248 | bytes 6586368 | tf_op jit(solution)/shard_map/while/body/eval_jaxpr/dot_general | solution.py:83
  34.0 1.6 %fusion.45 = f32[1728,128]{1,0:T(8,128)S(1)} fusion(bf16[1536,128]{1,0:T(8,128)(2,1)S(1)} %bitcast.78, bf16[216,8,12,128]{3,2,1,0:T(8,128)(2,1)S(1)} %bitcast.74), kind=kOutput, calls=%fused_computation.2.clone.1 | convolution fusion | flops 679477248 | bytes 6586368 | tf_op jit(solution)/shard_map/while/body/eval_jaxpr/dot_general | solution.py:84
  37.1 1.4 broadcast_compare_fusion.4
  38.5 5.9 %select_select_fusion.3 = (bf16[27,64,12,128]{3,2,1,0:T(8,128)(2,1)}, bf16[27,64,12,128]{3,2,1,0:T(8,128)(2,1)S(1)}) fusion(pred[64,12,128]{2,1,0:T(8,128)(4,1)S(1)} %get-tuple-element.305, pred[64,12,128]{2,1,0:T(8,128)(4,1)S(1)} %get-tuple-element.306, pred[64,12,128]{2,1,0:T(8,128)(4,1)S(1)} %get-tuple-element.307, ...), kind=kLoop, calls=%fused_computation.1.clone.1 | loop fusion | flops 15925248 | bytes 10939392 | tf_op jit(solution)/shard_map/while/body/eval_jaxpr/jit(_where)/select_n | solution.py:53
  45.5 4.6 %fusion.46 = f32[1728,128]{1,0:T(8,128)S(1)} fusion(bf16[1536,128]{1,0:T(8,128)(2,1)S(1)} %bitcast.77, bf16[216,8,12,128]{3,2,1,0:T(8,128)(2,1)} %bitcast.75), kind=kOutput, calls=%fused_computation.5.clone.1 | convolution fusion | flops 679477248 | bytes 6586368 | tf_op jit(solution)/shard_map/while/body/eval_jaxpr/dot_general | solution.py:83
  50.1 1.6 %fusion.45 = f32[1728,128]{1,0:T(8,128)S(1)} fusion(bf16[1536,128]{1,0:T(8,128)(2,1)S(1)} %bitcast.78, bf16[216,8,12,128]{3,2,1,0:T(8,128)(2,1)S(1)} %bitcast.74), kind=kOutput, calls=%fused_computation.2.clone.1 | convolution fusion | flops 679477248 | bytes 6586368 | tf_op jit(solution)/shard_map/while/body/eval_jaxpr/dot_general | solution.py:84
  53.2 1.4 broadcast_compare_fusion.4
  54.6 5.9 %select_select_fusion.3 = (bf16[27,64,12,128]{3,2,1,0:T(8,128)(2,1)}, bf16[27,64,12,128]{3,2,1,0:T(8,128)(2,1)S(1)}) fusion(pred[64,12,128]{2,1,0:T(8,128)(4,1)S(1)} %get-tuple-element.305, pred[64,12,128]{2,1,0:T(8,128)(4,1)S(1)} %get-tuple-element.306, pred[64,12,128]{2,1,0:T(8,128)(4,1)S(1)} %get-tuple-element.307, ...), kind=kLoop, calls=%fused_computation.1.clone.1 | loop fusion | flops 15925248 | bytes 10939392 | tf_op jit(solution)/shard_map/while/body/eval_jaxpr/jit(_where)/select_n | solution.py:53
  61.6 4.6 %fusion.46 = f32[1728,128]{1,0:T(8,128)S(1)} fusion(bf16[1536,128]{1,0:T(8,128)(2,1)S(1)} %bitcast.77, bf16[216,8,12,128]{3,2,1,0:T(8,128)(2,1)} %bitcast.75), kind=kOutput, calls=%fused_computation.5.clone.1 | convolution fusion | flops 679477248 | bytes 6586368 | tf_op jit(solution)/shard_map/while/body/eval_jaxpr/dot_general | solution.py:83
  66.2 1.6 %fusion.45 = f32[1728,128]{1,0:T(8,128)S(1)} fusion(bf16[1536,128]{1,0:T(8,128)(2,1)S(1)} %bitcast.78, bf16[216,8,12,128]{3,2,1,0:T(8,128)(2,1)S(1)} %bitcast.74), kind=kOutput, calls=%fused_computation.2.clone.1 | convolution fusion | flops 679477248 | bytes 6586368 | tf_op jit(solution)/shard_map/while/body/eval_jaxpr/dot_general | solution.py:84
  69.7 1.8 %reshape.564 = f32[32,1,6912]{2,1,0:T(1,128)S(1)} reshape(f32[32,1,2,27,2,64]{5,4,3,2,1,0:T(2,128)S(1)} %copy.33) | data formatting | bytes 1769472
  71.5 37.3 %all_to_all.15 = f32[32,1,6912]{2,1,0:T(1,128)S(1)} all-to-all(f32[32,1,6912]{2,1,0:T(1,128)S(1)} %reshape.564), channel_id=1, replica_groups=mesh['space'=32,'tm'=8] {'space'}, dimensions={0} | all-to-all | bytes 1769472 | tf_op jit(solution)/shard_map/all_to_all | solution.py:18
  109.4 2.8 %reduce.3 = f32[32,6912]{1,0:T(8,128)S(1)} reduce(f32[32,1,6912]{2,1,0:T(1,128)S(1)} %all_to_all.15, f32[]{:T(128)} %broadcast.901), dimensions={1}, to_apply=%all_to_all.9.reduce_sub_computation | reduce | bytes 1769476 | tf_op jit(solution)/shard_map/all_to_all | solution.py:18
  115.4 4.1 %all-to-all-start.1 = ((f32[8,1,6912]{2,1,0:T(1,128)}), f32[8,1,6912]{2,1,0:T(1,128)S(1)}, u32[]{:S(2)}, u32[]{:S(2)}) async-start(f32[8,1,6912]{2,1,0:T(1,128)} %reshape.566), calls=%async_computation.1 | async-start | bytes 442368 | tf_op jit(solution)/shard_map/all_to_all | solution.py:24
  119.6 5.6 %all-to-all-done.1 = f32[8,1,6912]{2,1,0:T(1,128)S(1)} async-done(((f32[8,1,6912]{2,1,0:T(1,128)}), f32[8,1,6912]{2,1,0:T(1,128)S(1)}, u32[]{:S(2)}, u32[]{:S(2)}) %all-to-all-start.1) | async-done | bytes 221216 | tf_op jit(solution)/shard_map/all_to_all | solution.py:24
  128.1 17.5 %all_to_all.16 = f32[32,1,432]{2,1,0:T(1,128)S(1)} all-to-all(f32[32,1,432]{2,1,0:T(1,128)S(1)} %reshape.568), channel_id=1, replica_groups=mesh['space'=32,'tm'=8] {'space'}, dimensions={0} | all-to-all | bytes 110592 | tf_op jit(solution)/shard_map/all_to_all | solution.py:24
  (62 shorter events, 19.1 us)
Async XLA Ops:
  0.6 3.8 %copy-start.1 = (s32[27,3]{0,1:T(4,128)S(1)}, s32[27,3]{0,1:T(4,128)}, u32[]{:S(2)}) copy-start(s32[27,3]{0,1:T(4,128)} %param.8) | copy-start | bytes 976
  109.4 10.2 %copy-start.2 = (s32[8,2]{0,1:T(2,128)S(1)}, s32[8,2]{0,1:T(2,128)}, u32[]{:S(2)}) copy-start(s32[8,2]{0,1:T(2,128)} %param.9) | copy-start | bytes 196
  114.1 32.6 %copy-start = (f32[2,27,2,64]{3,2,1,0:T(2,128)}, f32[2,27,2,64]{3,2,1,0:T(2,128)S(1)}, u32[]{:S(2)}) copy-start(f32[2,27,2,64]{3,2,1,0:T(2,128)S(1)} %reduce_sum.38) | copy-start | bytes 82948
  115.4 9.8 %all-to-all-start.1 = ((f32[8,1,6912]{2,1,0:T(1,128)}), f32[8,1,6912]{2,1,0:T(1,128)S(1)}, u32[]{:S(2)}, u32[]{:S(2)}) async-start(f32[8,1,6912]{2,1,0:T(1,128)} %reshape.566), calls=%async_computation.1 | async-start | bytes 442368 | tf_op jit(solution)/shard_map/all_to_all | solution.py:24
where the time goes:
time: 148 us; the launch traced here: 147 us
  blocking collectives  54.8 us (37%)
  other arithmetic  41.3 us (28%)
  matrix products  25.4 us (17%)
  local copies, waits for them, and re-layouts  15 us (10%)
  waiting for transfers between devices  5.6 us (4%)
  starting transfers between devices  4.13 us (3%)
    all_to_all x1, blocking collectives, summed_on_arrival(): lax.all_to_all(pieces, axis, split_axis=0, concat_axis=0, tiled=True)  37.3 us
    select_n x4, other arithmetic, phase_weights(): jnp.where(turns == 0, base_re, jnp.where(turns == 1, base_im, jnp.where(t...  23.8 us
    dot_general x4, matrix products, one_block(): left = jnp.dot(weight_re, stacked, preferred_element_type=jnp.float32)  18.3 us
    all_to_all x1, blocking collectives, copy_for_each(): return lax.all_to_all(copies, axis, split_axis=0, concat_axis=0, tiled=True)  17.5 us
    unnamed x16, local copies, waits for them, and re-layouts  9.55 us
    dot_general x4, matrix products, one_block(): right = jnp.dot(weight_im, stacked, preferred_element_type=jnp.float32)  6.3 us
    eq x4, other arithmetic, phase_weights(): turns == 0  5.79 us
    all_to_all x1, waiting for transfers between devices, copy_for_each(): return lax.all_to_all(copies, axis, split_axis=0, concat_axis=0, tiled=True)  5.6 us
  transfers between devices with their start and end apart: 1, of which 1 were waited for; matrix products, arithmetic and copies ran while one was open for 0% of the time, Pallas kernels for 0%

commit v1 on v0

v1 whole, which is shorter than its diff:
```python
import functools, math
import numpy as np
import jax, jax.numpy as jnp
from jax import lax
from jax.experimental import pallas as pl
from jax.experimental.pallas import tpu as pltpu
from jax.sharding import PartitionSpec as P

EXTENT = 48
S1, S2 = 1.625, 1.1325


def twiddles():
    table = np.zeros((3, 8, 128), np.float32)
    for ph in range(3):
        x = 16 * ph + np.arange(64)
        x = np.concatenate([x, x])
        a = 2 * np.pi * x / EXTENT
        table[ph, 0] = S1 * np.cos(a)
        table[ph, 1] = S1 * np.sin(a)
        table[ph, 2] = S2 * np.cos(2 * a)
        table[ph, 3] = S2 * np.sin(2 * a)
    return table


def turned(v):
    return jnp.concatenate([-v[:, 64:], v[:, :64]], axis=1)


def field_kernel(mom_ref, kap_ref, noise_ref, v_ref, tw_ref, out_ref, lhs, rhs, hrow):
    phase0 = lax.rem(lax.axis_index("space") * 32, 48)
    hrow[...] = jnp.zeros_like(hrow)

    def tile(lt, _):
        lane0 = pl.multiple_of(lt * 128, 128)
        for aq in range(3):
            n = [noise_ref[4 * aq + a, :, pl.ds(lane0, 128)].astype(jnp.float32).astype(jnp.bfloat16) for a in range(4)]
            for h in range(2):
                start = phase0 + lt * 128 + h * 64
                ph = lax.rem(start, 48) // 16
                tw = tw_ref[ph].astype(jnp.bfloat16)
                cut = slice(64 * h, 64 * h + 64)
                for pair in range(2):
                    both = jnp.concatenate([n[2 * pair][:, cut], n[2 * pair + 1][:, cut]], axis=1)
                    zr = jnp.abs(both - 2) - 1
                    zi = jnp.abs(both - 1) - 1
                    at = aq * 512 + pair * 128
                    for f in range(5):
                        rows = pl.ds(64 * f, 64)
                        if f == 0:
                            left, right = zr, zi
                        else:
                            w = tw[f - 1 : f, :]
                            if f % 2 == 1:
                                left, right = zr * w, zi * w
                            else:
                                left, right = zi * (-w), zr * w
                        lhs[h, rows, at : at + 128] = left
                        lhs[h, rows, at + 256 : at + 384] = right
                for a in range(4):
                    for g in range(4):
                        v = v_ref[4 * aq + a, pl.ds(pl.multiple_of(lt * 128 + h * 64 + 16 * g, 16), 16), :]
                        t = turned(v)
                        first = 16 * g < 48 - 16 * ph
                        zero = jnp.zeros_like(v)
                        at = aq * 512 + 64 * a + 16 * g
                        rhs[h, at : at + 16, 0:128] = jnp.where(first, v, zero)
                        rhs[h, at : at + 16, 128:256] = jnp.where(first, zero, v)
                        rhs[h, at + 256 : at + 272, 0:128] = jnp.where(first, t, zero)
                        rhs[h, at + 256 : at + 272, 128:256] = jnp.where(first, zero, t)
        for h in range(2):
            start = phase0 + lt * 128 + h * 64
            row = start // 48
            out = jnp.dot(lhs[h], rhs[h], preferred_element_type=jnp.float32)
            g = [out[64 * f : 64 * f + 64, :] for f in range(5)]
            terms = [g[3] + g[4], g[1] + g[2], g[0], g[1] - g[2], g[3] - g[4]]
            for q0 in range(5):
                for r in range(2):
                    hrow[q0, row + r] += terms[q0][:, 128 * r : 128 * r + 128]
        return 0

    lax.fori_loop(0, 4, tile, 0)

    def momentum(q, _):
        q0 = mom_ref[3 * q] + 2
        acc_r = jnp.zeros((64, 128), jnp.float32)
        acc_i = jnp.zeros((64, 128), jnp.float32)
        for row in range(12):
            part = hrow[q0, row]
            acc_r += kap_ref[24 * q + 2 * row] * part
            acc_i += kap_ref[24 * q + 2 * row + 1] * part
        out_ref[q] = acc_r + turned(acc_i)
        return 0

    lax.fori_loop(0, 27, momentum, 0)


def row_phases(momenta, scale):
    first = lax.axis_index("space") * 512 // EXTENT
    row = first + jnp.arange(12, dtype=jnp.int32)
    y, z = row % EXTENT, row // EXTENT
    m = (momenta[:, 1:2] * y + momenta[:, 2:3] * z) % EXTENT
    angle = m.astype(jnp.float32) * jnp.float32(2.0 * math.pi / EXTENT)
    q0 = jnp.abs(momenta[:, 0:1])
    size = jnp.where(q0 == 0, scale, jnp.where(q0 == 1, scale / S1, scale / S2)).astype(jnp.float32)
    return jnp.stack([jnp.cos(angle) * size, -jnp.sin(angle) * size], axis=2)


def partial_field(solutions, noise, momenta, scale):
    kap = row_phases(momenta, scale).reshape(-1)
    vmem = pl.BlockSpec(memory_space=pltpu.VMEM)
    smem = pl.BlockSpec(memory_space=pltpu.SMEM)
    return pl.pallas_call(
        field_kernel,
        out_shape=jax.ShapeDtypeStruct((27, 64, 128), jnp.float32),
        in_specs=[smem, smem, vmem, vmem, vmem],
        out_specs=vmem,
        scratch_shapes=[
            pltpu.VMEM((2, 320, 1536), jnp.bfloat16),
            pltpu.VMEM((2, 1536, 256), jnp.bfloat16),
            pltpu.VMEM((5, 12, 64, 128), jnp.float32),
        ],
        compiler_params=pltpu.CompilerParams(vmem_limit_bytes=40 * 1024 * 1024),
        name="fields",
    )(momenta.reshape(-1), kap, noise.transpose(1, 0, 2), solutions, jnp.asarray(twiddles()))


def in_blocks(array, dim, length):
    before, after = (array.shape[:dim], array.shape[dim + 1 :])
    return jnp.moveaxis(array.reshape(*before, length, -1, *after), dim, 0)


def summed_on_arrival(array, axis, dim):
    pieces = in_blocks(array, dim, lax.axis_size(axis))
    arrived = lax.all_to_all(pieces, axis, split_axis=0, concat_axis=0, tiled=True)
    return arrived.sum(axis=0)


def copy_for_each(array, axis):
    copies = jnp.broadcast_to(array, (lax.axis_size(axis), *array.shape))
    return lax.all_to_all(copies, axis, split_axis=0, concat_axis=0, tiled=True)


def laid_out(pieces, dim):
    pieces = jnp.moveaxis(pieces, 0, dim)
    dims = pieces.shape
    return pieces.reshape(*dims[:dim], dims[dim] * dims[dim + 1], *dims[dim + 2 :])


def gathered_copies(array, axis, dim):
    pieces = copy_for_each(array, axis)
    return laid_out(pieces, dim)


def over_copies(array, axis):
    return copy_for_each(array, axis).sum(axis=0)


def pair_traces(fields, pairs):
    nslices = fields.shape[0]
    slots = jnp.arange(nslices, dtype=jnp.int32)
    pick_sink = (pairs[:, 1][:, None] == slots[None, :]).astype(jnp.float32)
    pick_source = (pairs[:, 0][:, None] == slots[None, :]).astype(jnp.float32)
    sink = jnp.einsum("kt,tcpij->kcpij", pick_sink, fields, precision=lax.Precision.HIGHEST)
    source = jnp.einsum("kt,tcpij->kcpij", pick_source, fields, precision=lax.Precision.HIGHEST)
    real_part = jnp.sum(sink[:, 0] * source[:, 0] + sink[:, 1] * source[:, 1], axis=(2, 3))
    imag_part = jnp.sum(sink[:, 1] * source[:, 0] - sink[:, 0] * source[:, 1], axis=(2, 3))
    return jnp.stack([real_part, imag_part], 1)


def local(solutions, noise, momenta, pairs):
    nvec = noise.shape[1]
    scale = 1.0 / math.sqrt(noise.shape[2] * solutions.shape[2] * lax.axis_size("space"))
    field = partial_field(solutions[0], noise[0], momenta, scale)
    pieces = field.reshape(27, 32, 2, 128).transpose(1, 0, 2, 3).reshape(32, 54, 128)
    arrived = lax.all_to_all(pieces, "space", split_axis=0, concat_axis=0, tiled=True).sum(axis=0)
    mesons = arrived.reshape(27, 2, 2, 64).transpose(2, 0, 1, 3)[None]
    every_slice = gathered_copies(mesons, "tm", 0)
    partial_traces = pair_traces(every_slice, pairs)
    correlators = over_copies(partial_traces, "space") / nvec
    return (mesons, correlators)


def solution(mesh):
    in_specs = (P("tm", None, "space", None), P("tm", None, None, "space"), P(), P("tm", None))
    out_specs = (P("tm", None, None, "space", None), P("tm", None, None))
    return jax.shard_map(local, mesh=mesh, in_specs=in_specs, out_specs=out_specs, check_vma=False)
```

time: 148 us -> 88.7 us (0.60)
  other arithmetic: 41.3 us -> 3.26 us
  matrix products: 25.4 us -> 0.76 us
  blocking collectives: 54.8 us -> 37.8 us
  waiting for transfers between devices: 5.6 us -> 14.7 us
  starting transfers between devices: 4.13 us -> 12.1 us
  Pallas kernels: 0 us -> 7.74 us
  local copies, waits for them, and re-layouts: 15 us -> 11 us
    dot_general x8 -> x0, matrix products: 24.6 us -> none  [the longest x4 18.3 us: one_block(): left = jnp.dot(weight_re, stacked, preferred_element_type=jnp.float32)]
    select_n x12 -> x1, other arithmetic: 23.9 us -> 0.01 us  [row_phases(): y, z = (row % EXTENT, row // EXTENT)]
    all_to_all x2 -> x1, blocking collectives: 54.8 us -> 37.8 us  [local(): lax.all_to_all(pieces, 'space', split_axis=0, concat_axis=0, tiled=True)]
    all_to_all x1 -> x2, waiting for transfers between devices: 5.6 us -> 14.7 us  [copy_for_each(): return lax.all_to_all(copies, axis, split_axis=0, concat_axis=0, tiled=True)]
    all_to_all x1 -> x2, starting transfers between devices: 4.13 us -> 12.1 us  [copy_for_each(): return lax.all_to_all(copies, axis, split_axis=0, concat_axis=0, tiled=True)]
    pallas_call x0 -> x1, Pallas kernels: none -> 7.74 us  [partial_field(): pl.pallas_call(field_kernel, out_shape=jax.ShapeDtypeStruct((27, 64, 128)...]
    eq x4 -> x0, other arithmetic: 5.79 us -> none  [phase_weights(): turns == 0]
    dynamic_slice x4 -> x0, local copies, waits for them, and re-layouts: 4.09 us -> none  [one_block(): vec_block = lax.dynamic_slice_in_dim(vectors, first, block, 1)]
  transfers between devices with their start and end apart: 1 -> 2, of which waited for: 1 -> 2; matrix products, arithmetic and copies ran while one was open for 0% -> 1% of each run, Pallas kernels for 0% -> 0%
where the time goes in v1:
time: 88.7 us; the launch traced here: 88.2 us
  blocking collectives  37.8 us (43%)
  waiting for transfers between devices  14.7 us (17%)
  starting transfers between devices  12.1 us (14%)
  local copies, waits for them, and re-layouts  11 us (12%)
  Pallas kernels  7.74 us (9%)
  other arithmetic  3.26 us (4%)
    all_to_all x1, blocking collectives, local(): lax.all_to_all(pieces, 'space', split_axis=0, concat_axis=0, tiled=True)  37.8 us
    all_to_all x2, waiting for transfers between devices, copy_for_each(): return lax.all_to_all(copies, axis, split_axis=0, concat_axis=0, tiled=True)  14.7 us
    all_to_all x2, starting transfers between devices, copy_for_each(): return lax.all_to_all(copies, axis, split_axis=0, concat_axis=0, tiled=True)  12.1 us
    unnamed x17, local copies, waits for them, and re-layouts  8.35 us
    pallas_call x1, Pallas kernels, partial_field(): pl.pallas_call(field_kernel, out_shape=jax.ShapeDtypeStruct((27, 64, 128)...  7.74 us
    all_to_all x2, other arithmetic, copy_for_each(): return lax.all_to_all(copies, axis, split_axis=0, concat_axis=0, tiled=True)  1.96 us
  transfers between devices with their start and end apart: 2, of which 2 were waited for; matrix products, arithmetic and copies ran while one was open for 1% of the time, Pallas kernels for 0%

profile of v1, /device:TPU:1, one launch (start us, length us, event | category | flops | bytes accessed | tf_op | source)
XLA Modules:
  0.0 88.2 jit_solution(13683518116141149549)
XLA Ops:
  0.6 0.8 slice_bitcast_fusion.3
  1.4 0.7 fusion.14
  2.1 0.8 copy.49
  2.9 0.3 cosine_multiply_fusion
  3.7 1.4 %copy-done = s32[1,64,12,512]{3,1,2,0:T(8,128)S(1)} copy-done((s32[1,64,12,512]{3,1,2,0:T(8,128)S(1)}, s32[1,64,12,512]{3,1,2,0:T(8,128)}, u32[]{:S(2)}) %copy-start) | copy-done | bytes 1572888
  5.1 1.4 %copy-done.1 = bf16[1,12,512,128]{3,2,1,0:T(8,128)(2,1)S(1)} copy-done((bf16[1,12,512,128]{3,2,1,0:T(8,128)(2,1)S(1)}, bf16[1,12,512,128]{3,2,1,0:T(8,128)(2,1)}, u32[]{:S(2)}) %copy-start.1) | copy-done | bytes 1572888
  6.5 0.7 copy-done.2
  7.2 7.7 %fields.1 = f32[27,64,128]{2,1,0:T(8,128)S(1)} custom-call(s32[81]{0:T(128)S(1)} %reshape.314.mom_ref, f32[648]{0:T(1024)S(1)} %reshape.315.kap_ref, s32[12,64,512]{2,1,0:T(8,128)S(1)} %bitcast.43, bf16[12,512,128]{2,1,0:T(8,128)(2,1)S(1)} %bitcast.44, f32[3,8,128]{2,1,0:T(8,128)S(1)} %copy-done.2), custom_call_target="tpu_custom_call" | custom-call | tf_op jit(solution)/shard_map/fields/pallas_call | solution.py:113
  15.1 0.5 copy.52
  15.6 37.8 %all_to_all.15 = f32[32,54,128]{2,1,0:T(8,128)S(1)} all-to-all(f32[32,54,128]{2,1,0:T(8,128)S(1)} %copy.52), channel_id=1, replica_groups=mesh['space'=32,'tm'=8] {'space'}, dimensions={0} | all-to-all | bytes 1769472 | tf_op jit(solution)/shard_map/all_to_all | solution.py:176
  53.8 1.1 %reshape.322 = f32[8,1,6912]{2,1,0:T(1,128)} reshape(f32[8,1,2,27,2,64]{5,4,3,2,1,0:T(2,128)S(1)} %broadcast_in_dim.29) | data formatting | bytes 442368
  54.9 4.1 %all-to-all-start.1 = ((f32[8,1,6912]{2,1,0:T(1,128)}), f32[8,1,6912]{2,1,0:T(1,128)S(1)}, u32[]{:S(2)}, u32[]{:S(2)}) async-start(f32[8,1,6912]{2,1,0:T(1,128)} %reshape.322), calls=%async_computation.1 | async-start | bytes 442368 | tf_op jit(solution)/shard_map/all_to_all | solution.py:141
  59.0 5.6 %all-to-all-done.1 = f32[8,1,6912]{2,1,0:T(1,128)S(1)} async-done(((f32[8,1,6912]{2,1,0:T(1,128)}), f32[8,1,6912]{2,1,0:T(1,128)S(1)}, u32[]{:S(2)}, u32[]{:S(2)}) %all-to-all-start.1) | async-done | bytes 221216 | tf_op jit(solution)/shard_map/all_to_all | solution.py:141
  64.6 0.5 broadcast.283
  65.2 1.2 %reduce.2 = f32[8,6912]{1,0:T(8,128)S(1)} reduce(f32[8,1,6912]{2,1,0:T(1,128)S(1)} %all-to-all-done.1, f32[]{:T(128)} %broadcast.283), dimensions={1}, to_apply=%all_to_all.10.reduce_sub_computation | reduce | bytes 442372 | tf_op jit(solution)/shard_map/all_to_all | solution.py:141
  66.3 0.3 reshape.323
  66.6 0.4 fusion
  67.0 0.4 fusion.2
  67.7 1.0 %reshape.324 = f32[32,1,432]{2,1,0:T(1,128)} reshape(f32[32,2,8,27]{3,2,1,0:T(8,128)S(1)} %broadcast_bitcast_fusion) | data formatting | bytes 110592
  68.7 7.9 %all-to-all-start.2 = ((f32[32,1,432]{2,1,0:T(1,128)}), f32[32,1,432]{2,1,0:T(1,128)S(1)}, u32[]{:S(2)}, u32[]{:S(2)}) async-start(f32[32,1,432]{2,1,0:T(1,128)} %reshape.324), calls=%async_computation.2 | async-start | bytes 131072 | tf_op jit(solution)/shard_map/all_to_all | solution.py:141
  76.6 0.7 copy.57
  77.3 9.1 %all-to-all-done.2 = f32[32,1,432]{2,1,0:T(1,128)S(1)} async-done(((f32[32,1,432]{2,1,0:T(1,128)}), f32[32,1,432]{2,1,0:T(1,128)S(1)}, u32[]{:S(2)}, u32[]{:S(2)}) %all-to-all-start.2) | async-done | bytes 55328 | tf_op jit(solution)/shard_map/all_to_all | solution.py:141
  86.4 0.8 reduce.3
  87.5 0.7 copy.58
  (24 shorter events, 1.5 us)
Async XLA Ops:
  3.7 1.4 %copy-start = (s32[1,64,12,512]{3,1,2,0:T(8,128)S(1)}, s32[1,64,12,512]{3,1,2,0:T(8,128)}, u32[]{:S(2)}) copy-start(s32[1,64,12,512]{3,1,2,0:T(8,128)} %param.6) | copy-start | bytes 4718596
  5.1 1.4 %copy-start.1 = (bf16[1,12,512,128]{3,2,1,0:T(8,128)(2,1)S(1)}, bf16[1,12,512,128]{3,2,1,0:T(8,128)(2,1)}, u32[]{:S(2)}) copy-start(bf16[1,12,512,128]{3,2,1,0:T(8,128)(2,1)} %param.5) | copy-start | bytes 4718596
  6.5 0.7 copy-start.2
  53.4 5.6 %copy-start.3 = (s32[8,2]{0,1:T(2,128)S(1)}, s32[8,2]{0,1:T(2,128)}, u32[]{:S(2)}) copy-start(s32[8,2]{0,1:T(2,128)} %param.8) | copy-start | bytes 196
  54.9 9.7 %all-to-all-start.1 = ((f32[8,1,6912]{2,1,0:T(1,128)}), f32[8,1,6912]{2,1,0:T(1,128)S(1)}, u32[]{:S(2)}, u32[]{:S(2)}) async-start(f32[8,1,6912]{2,1,0:T(1,128)} %reshape.322), calls=%async_computation.1 | async-start | bytes 442368 | tf_op jit(solution)/shard_map/all_to_all | solution.py:141
  68.7 17.7 %all-to-all-start.2 = ((f32[32,1,432]{2,1,0:T(1,128)}), f32[32,1,432]{2,1,0:T(1,128)S(1)}, u32[]{:S(2)}, u32[]{:S(2)}) async-start(f32[32,1,432]{2,1,0:T(1,128)} %reshape.324), calls=%async_computation.2 | async-start | bytes 131072 | tf_op jit(solution)/shard_map/all_to_all | solution.py:141

commit v2 on v0

v2 whole, which is shorter than its diff:
```python
import math

import jax
import jax.numpy as jnp
from jax import lax
from jax.experimental import pallas as pl
from jax.experimental.pallas import tpu as pltpu
from jax.sharding import PartitionSpec as P

EXTENT = 48
MOMS = 27
CHUNKS = 7
SIZE1, SIZE2 = 1.625, 1.1325
MESH = pl.DeviceIdType.MESH


def iota(shape, dim):
    return lax.broadcasted_iota(jnp.int32, shape, dim)


def swap_halves(array):
    return jnp.concatenate([array[:, 64:], array[:, :64]], axis=1)


def swapped(low, high, bit):
    has_bit = (iota((8, 128), 0) & bit) != 0
    return (
        jnp.where(has_bit, pltpu.roll(high, bit, 0), low),
        jnp.where(has_bit, high, pltpu.roll(low, 8 - bit, 0)),
    )


def fields_kernel(
    mom_s, pair_s, mom_v, noise_h, vec_h, mesons, traces,
    noise_v, vec_v, lhs, rhs, hrow, kap_r, kap_i,
    raw, core_in, half, y_in, own, z_in, slices, here, turned, four, eight,
    noise_sem, vec_sem, core_s, core_r, y_s, y_r, z_s, z_r, t_s, t_r, four_s, four_r, eight_s, eight_r,
):
    space, tm = lax.axis_index("space"), lax.axis_index("tm")
    z, y, core = space // 4, lax.rem(space // 2, 2), lax.rem(space, 2)
    quad = lax.rem(space, 4)

    def in_z(d):
        return {"space": lax.rem(z + d, 8) * 4 + quad, "tm": tm}

    def in_quad(d):
        return {"space": z * 4 + (quad ^ d), "tm": tm}

    def in_tm(d):
        return {"space": space, "tm": lax.rem(tm + d, 8)}

    def load(tile):
        lanes = pl.ds(tile * 128, 128)
        return (
            pltpu.make_async_copy(noise_h.at[:, :, lanes], noise_v.at[tile], noise_sem.at[tile]),
            pltpu.make_async_copy(vec_h.at[:, lanes, :], vec_v.at[tile], vec_sem.at[tile]),
        )

    for tile in range(4):
        for copy in load(tile):
            copy.start()

    barrier = pltpu.get_barrier_semaphore()
    for d in range(1, 4):
        pl.semaphore_signal(barrier, inc=1, device_id=in_quad(d), device_id_type=MESH)
    for d in range(1, 8):
        pl.semaphore_signal(barrier, inc=1, device_id=in_z(d), device_id_type=MESH)
        pl.semaphore_signal(barrier, inc=1, device_id=in_tm(d), device_id_type=MESH)

    scale = 1.0 / math.sqrt(12 * 512 * 32)
    row = space * 512 // EXTENT + iota((MOMS, 128), 1)
    q0 = jnp.abs(mom_v[:, 0:1])
    angle = (mom_v[:, 1:2] * lax.rem(row, EXTENT) + mom_v[:, 2:3] * (row // EXTENT)).astype(jnp.float32)
    angle = angle * jnp.float32(2.0 * math.pi / EXTENT)
    size = jnp.where(q0 == 0, scale, jnp.where(q0 == 1, scale / SIZE1, scale / SIZE2))
    phase_r, phase_i = jnp.cos(angle) * size, -jnp.sin(angle) * size
    left = iota((MOMS, 128), 1) < 64
    for r in range(12):
        kap_r[r] = jnp.broadcast_to(phase_r[:, r : r + 1], (MOMS, 128))
        column = jnp.broadcast_to(phase_i[:, r : r + 1], (MOMS, 128))
        kap_i[r] = jnp.where(left, column, -column)

    hrow[...] = jnp.zeros_like(hrow)
    phase0 = lax.rem(space * 32, EXTENT)
    lane = lax.rem(iota((8, 128), 1), 64)
    kind = iota((8, 128), 0)
    harmonic = jnp.where(kind < 2, 1, 2)
    amplitude = jnp.where(kind < 2, SIZE1, SIZE2)
    negate = iota((16, 128), 1) < 64

    def tile_step(tile, _):
        for copy in load(tile):
            copy.wait()
        starts = [phase0 + tile * 128 + 64 * h for h in range(2)]
        firsts = [lax.rem(start, EXTENT) for start in starts]
        waves = []
        for first in firsts:
            turn = ((first + lane) * harmonic).astype(jnp.float32) * jnp.float32(2.0 * math.pi / EXTENT)
            waves.append((amplitude * jnp.where(kind % 2 == 0, jnp.cos(turn), jnp.sin(turn))).astype(jnp.bfloat16))
        for a4 in range(3):
            n = [noise_v[tile, 4 * a4 + a].astype(jnp.float32).astype(jnp.bfloat16) for a in range(4)]
            for h in range(2):
                cut = slice(64 * h, 64 * h + 64)
                for two in range(2):
                    both = jnp.concatenate([n[2 * two][:, cut], n[2 * two + 1][:, cut]], axis=1)
                    z4_r, z4_i = jnp.abs(both - 2) - 1, jnp.abs(both - 1) - 1
                    at = a4 * 512 + two * 128
                    for f in range(5):
                        rows = pl.ds(64 * f, 64)
                        if f == 0:
                            first_part, second_part = z4_r, z4_i
                        else:
                            wave = waves[h][f - 1 : f, :]
                            if f % 2 == 1:
                                first_part, second_part = z4_r * wave, z4_i * wave
                            else:
                                first_part, second_part = z4_i * (-wave), z4_r * wave
                        lhs[h, rows, at : at + 128] = first_part
                        lhs[h, rows, at + 256 : at + 384] = second_part
                for a in range(4):
                    for g in range(4):
                        v = vec_v[tile, 4 * a4 + a, 64 * h + 16 * g : 64 * h + 16 * g + 16, :]
                        t = swap_halves(v)
                        t = jnp.where(negate, -t, t)
                        in_first = firsts[h] + 16 * g < EXTENT
                        zero = jnp.zeros_like(v)
                        at = a4 * 512 + 64 * a + 16 * g
                        rhs[h, at : at + 16, 0:128] = jnp.where(in_first, v, zero)
                        rhs[h, at : at + 16, 128:256] = jnp.where(in_first, zero, v)
                        rhs[h, at + 256 : at + 272, 0:128] = jnp.where(in_first, t, zero)
                        rhs[h, at + 256 : at + 272, 128:256] = jnp.where(in_first, zero, t)
        for h in range(2):
            out = jnp.dot(lhs[h], rhs[h], preferred_element_type=jnp.float32)
            f = [out[64 * k : 64 * k + 64, :] for k in range(5)]
            terms = [f[3] + f[4], f[1] + f[2], f[0], f[1] - f[2], f[3] - f[4]]
            for k in range(5):
                for r in range(2):
                    hrow[k, starts[h] // EXTENT + r] += terms[k][:, 128 * r : 128 * r + 128]
        return 0

    lax.fori_loop(0, 4, tile_step, 0)
    pl.semaphore_wait(barrier, 17)

    def to_core(g):
        return pltpu.make_async_remote_copy(
            src_ref=raw.at[1 - core, g], dst_ref=core_in.at[g], send_sem=core_s.at[g], recv_sem=core_r.at[g],
            device_id=in_quad(1), device_id_type=MESH,
        )

    def to_y(g):
        return pltpu.make_async_remote_copy(
            src_ref=half.at[g, 1 - y], dst_ref=y_in.at[g], send_sem=y_s.at[g], recv_sem=y_r.at[g],
            device_id=in_quad(2), device_id_type=MESH,
        )

    def to_z(g, d):
        return pltpu.make_async_remote_copy(
            src_ref=own.at[g, lax.rem(z + d, 8)], dst_ref=z_in.at[g, d - 1],
            send_sem=z_s.at[g, d - 1], recv_sem=z_r.at[g, d - 1], device_id=in_z(d), device_id_type=MESH,
        )

    def to_tm(g, d):
        return pltpu.make_async_remote_copy(
            src_ref=slices.at[g, tm], dst_ref=slices.at[g, tm],
            send_sem=t_s.at[g, d - 1], recv_sem=t_r.at[g, d - 1], device_id=in_tm(d), device_id_type=MESH,
        )

    def momentum(g, k):
        q = lax.min(4 * g + k, MOMS - 1)
        q0 = mom_s[0, q] + 2
        acc_r = [jnp.zeros((8, 128), jnp.float32) for _ in range(8)]
        acc_i = [jnp.zeros((8, 128), jnp.float32) for _ in range(8)]
        for r in range(12):
            k_r = jnp.broadcast_to(kap_r[r, pl.ds(q, 1), :], (8, 128))
            k_i = jnp.broadcast_to(kap_i[r, pl.ds(q, 1), :], (8, 128))
            for i in range(8):
                part = hrow[q0, r, 8 * i : 8 * i + 8, :]
                acc_r[i] += k_r * part
                acc_i[i] += k_i * part
        tiles = [acc_r[i] + swap_halves(acc_i[i]) for i in range(8)]
        by_core = [swapped(tiles[2 * i], tiles[2 * i + 1], 2) for i in range(4)]
        for c in range(2):
            for i in range(2):
                by_y = swapped(by_core[2 * i][c], by_core[2 * i + 1][c], 4)
                for yy in range(2):
                    raw[c, g, yy, k, 8 * i : 8 * i + 8, :] = by_y[yy]

    def after_core(g):
        to_core(g).wait_recv()
        for yy in range(2):
            half[g, yy] = raw[core, g, yy] + core_in[g, yy]
        to_y(g).start()

    def first_step(g, _):
        def one(k, _):
            momentum(g, k)
            return 0

        lax.fori_loop(0, 4, one, 0)
        to_core(g).start()

        @pl.when(g >= 1)
        def _():
            after_core(g - 1)

        return 0

    lax.fori_loop(0, CHUNKS, first_step, 0)
    after_core(CHUNKS - 1)

    def after_y(g, _):
        to_y(g).wait_recv()
        sums = half[g, y] + y_in[g]
        for top in range(2):
            tiles = [sums[k, 8 * top : 8 * top + 8, :] for k in range(4)]
            low = [swapped(tiles[2 * k], tiles[2 * k + 1], 2) for k in range(2)]
            for bit in range(2):
                pair = swapped(low[0][bit], low[1][bit], 4)
                for upper in range(2):
                    own[g, 4 * top + 2 * upper + bit] = pair[upper]
        for d in range(1, 8):
            to_z(g, d).start()
        return 0

    lax.fori_loop(0, CHUNKS, after_y, 0)

    def after_z(g, _):
        total = own[g, z]
        for d in range(1, 8):
            to_z(g, d).wait_recv()
            total += z_in[g, d - 1]
        mesons[g] = total
        slices[g, tm] = total
        for d in range(1, 8):
            to_tm(g, d).start()
        return 0

    lax.fori_loop(0, CHUNKS, after_z, 0)

    lanes = iota((8, 128), 1)

    def after_tm(g, sums):
        for d in range(1, 8):
            to_tm(g, d).wait_recv()
        for t in range(8):
            tile = slices[g, t]
            here[t] = tile
            turned[t] = swap_halves(jnp.where(lanes < 64, tile, -tile))
        for k in range(8):
            sink, source, rotated = here[pair_s[1, k]], here[pair_s[0, k]], turned[pair_s[0, k]]
            for c, term in enumerate((sink * source, sink * rotated)):
                value = jnp.sum(term, axis=1, keepdims=True)
                sums = jnp.where(lanes == (2 * k + c) * CHUNKS + g, value, sums)
        return sums

    four[quad] = lax.fori_loop(0, CHUNKS, after_tm, jnp.zeros((8, 128), jnp.float32))

    def to_quad(d):
        return pltpu.make_async_remote_copy(
            src_ref=four.at[quad], dst_ref=four.at[quad], send_sem=four_s.at[d - 1], recv_sem=four_r.at[d - 1],
            device_id=in_quad(d), device_id_type=MESH,
        )

    def to_all_z(d):
        return pltpu.make_async_remote_copy(
            src_ref=eight.at[z], dst_ref=eight.at[z], send_sem=eight_s.at[d - 1], recv_sem=eight_r.at[d - 1],
            device_id=in_z(d), device_id_type=MESH,
        )

    for d in range(1, 4):
        to_quad(d).start()
    for d in range(1, 4):
        to_quad(d).wait_recv()
    eight[z] = (four[0] + four[1]) + (four[2] + four[3])
    for d in range(1, 8):
        to_all_z(d).start()
    for d in range(1, 8):
        to_all_z(d).wait_recv()
    total = eight[0]
    for k in range(1, 8):
        total += eight[k]
    traces[...] = total * (1.0 / 64)

    def finish(g, _):
        to_core(g).wait_send()
        to_y(g).wait_send()
        for d in range(1, 8):
            to_z(g, d).wait_send()
            to_tm(g, d).wait_send()
        return 0

    lax.fori_loop(0, CHUNKS, finish, 0)
    for d in range(1, 4):
        to_quad(d).wait_send()
    for d in range(1, 8):
        to_all_z(d).wait_send()


def local(solutions, noise, momenta, pairs):
    f32, bf16 = jnp.float32, jnp.bfloat16
    vmem = pl.BlockSpec(memory_space=pltpu.VMEM)
    smem = pl.BlockSpec(memory_space=pltpu.SMEM)
    hbm = pl.BlockSpec(memory_space=pl.ANY)
    dma = pltpu.SemaphoreType.DMA
    mesons, traces = pl.pallas_call(
        fields_kernel,
        out_shape=(
            jax.ShapeDtypeStruct((CHUNKS, 8, 128), f32),
            jax.ShapeDtypeStruct((8, 128), f32),
        ),
        in_specs=[smem, smem, vmem, hbm, hbm],
        out_specs=(vmem, vmem),
        scratch_shapes=[
            pltpu.VMEM((4, 12, 64, 128), jnp.int32),
            pltpu.VMEM((4, 12, 128, 128), bf16),
            pltpu.VMEM((2, 320, 1536), bf16),
            pltpu.VMEM((2, 1536, 256), bf16),
            pltpu.VMEM((5, 12, 64, 128), f32),
            pltpu.VMEM((12, MOMS, 128), f32),
            pltpu.VMEM((12, MOMS, 128), f32),
            pltpu.VMEM((2, CHUNKS, 2, 4, 16, 128), f32),
            pltpu.VMEM((CHUNKS, 2, 4, 16, 128), f32),
            pltpu.VMEM((CHUNKS, 2, 4, 16, 128), f32),
            pltpu.VMEM((CHUNKS, 4, 16, 128), f32),
            pltpu.VMEM((CHUNKS, 8, 8, 128), f32),
            pltpu.VMEM((CHUNKS, 7, 8, 128), f32),
            pltpu.VMEM((CHUNKS, 8, 8, 128), f32),
            pltpu.VMEM((8, 8, 128), f32),
            pltpu.VMEM((8, 8, 128), f32),
            pltpu.VMEM((4, 8, 128), f32),
            pltpu.VMEM((8, 8, 128), f32),
            dma((4,)), dma((4,)),
            dma((CHUNKS,)), dma((CHUNKS,)),
            dma((CHUNKS,)), dma((CHUNKS,)),
            dma((CHUNKS, 7)), dma((CHUNKS, 7)),
            dma((CHUNKS, 7)), dma((CHUNKS, 7)),
            dma((3,)), dma((3,)),
            dma((7,)), dma((7,)),
        ],
        compiler_params=pltpu.CompilerParams(
            collective_id=0, has_side_effects=True, vmem_limit_bytes=40 * 1024 * 1024
        ),
        name="meson_fields",
    )(momenta.T, pairs.T, momenta, noise[0].transpose(1, 0, 2), solutions[0])
    mesons = mesons.reshape(4 * CHUNKS, 2, 2, 64)[:MOMS].transpose(2, 0, 1, 3)[None]
    traces = traces.reshape(4, 2, 128).sum(axis=1)[:, : 16 * CHUNKS].reshape(4, 16, CHUNKS)
    correlators = traces.transpose(1, 2, 0).reshape(8, 2, 4 * CHUNKS)[:, :, :MOMS]
    return (mesons, correlators)


def solution(mesh):
    in_specs = (P("tm", None, "space", None), P("tm", None, None, "space"), P(), P("tm", None))
    out_specs = (P("tm", None, None, "space", None), P("tm", None, None))
    return jax.shard_map(local, mesh=mesh, in_specs=in_specs, out_specs=out_specs, check_vma=False)
```

time: 148 us -> 48 us (0.32)
  blocking collectives: 54.8 us -> 0 us
  other arithmetic: 41.3 us -> 0.02 us
  Pallas kernels: 0 us -> 40.5 us
  matrix products: 25.4 us -> 0 us
  local copies, waits for them, and re-layouts: 15 us -> 6.68 us
  waiting for transfers between devices: 5.6 us -> 0 us
  starting transfers between devices: 4.13 us -> 0 us
    all_to_all x2 -> x0, blocking collectives: 54.8 us -> none  [the longest x1 37.3 us: summed_on_arrival(): lax.all_to_all(pieces, axis, split_axis=0, concat_axis=0, tiled=True)]
    pallas_call x0 -> x1, Pallas kernels: none -> 40.5 us  [local(): pl.pallas_call(fields_kernel, out_shape=(jax.ShapeDtypeStruct((CHUNKS, 8,...]
    dot_general x10 -> x0, matrix products: 25.4 us -> none  [the longest x4 18.3 us: one_block(): left = jnp.dot(weight_re, stacked, preferred_element_type=jnp.float32)]
    select_n x12 -> x0, other arithmetic: 23.9 us -> none  [the longest x4 23.8 us: phase_weights(): jnp.where(turns == 0, base_re, jnp.where(turns == 1, base_im, jnp.where(t...]
    eq x4 -> x0, other arithmetic: 5.79 us -> none  [phase_weights(): turns == 0]
    all_to_all x1 -> x0, waiting for transfers between devices: 5.6 us -> none  [copy_for_each(): return lax.all_to_all(copies, axis, split_axis=0, concat_axis=0, tiled=True)]
    all_to_all x3 -> x0, other arithmetic: 4.71 us -> none  [the longest x1 2.75 us: summed_on_arrival(): lax.all_to_all(pieces, axis, split_axis=0, concat_axis=0, tiled=True)]
    all_to_all x1 -> x0, starting transfers between devices: 4.13 us -> none  [copy_for_each(): return lax.all_to_all(copies, axis, split_axis=0, concat_axis=0, tiled=True)]
  transfers between devices with their start and end apart: 1 -> 0, of which waited for: 1 -> 0; matrix products, arithmetic and copies ran while one was open for 0% -> 0% of each run, Pallas kernels for 0% -> 0%
where the time goes in v2:
time: 48 us; the launch traced here: 47.8 us
  Pallas kernels  40.5 us (84%)
  local copies, waits for them, and re-layouts  6.68 us (14%)
  between operations  0.67 us (1%)
    pallas_call x1, Pallas kernels, local(): pl.pallas_call(fields_kernel, out_shape=(jax.ShapeDtypeStruct((CHUNKS, 8,...  40.5 us
    unnamed x10, local copies, waits for them, and re-layouts  5.6 us

profile of v2, /device:TPU:1, one launch (start us, length us, event | category | flops | bytes accessed | tf_op | source)
XLA Modules:
  0.0 47.8 jit_solution(7483664087314562576)
XLA Ops:
  0.6 0.8 %copy.8.mom_v = s32[27,3]{1,0:T(8,128)S(1)} copy(s32[27,3]{0,1:T(4,128)} %param.6) | data formatting | bytes 648 | tf_op args[2]
  1.4 0.0 copy-start
  1.4 1.4 %copy-done = s32[1,64,12,512]{3,1,2,0:T(8,128)S(1)} copy-done((s32[1,64,12,512]{3,1,2,0:T(8,128)S(1)}, s32[1,64,12,512]{3,1,2,0:T(8,128)}, u32[]{:S(2)}) %copy-start) | copy-done | bytes 1572888
  2.8 0.0 copy-start.1
  2.8 1.4 %copy-done.1 = bf16[1,12,512,128]{3,2,1,0:T(8,128)(2,1)S(1)} copy-done((bf16[1,12,512,128]{3,2,1,0:T(8,128)(2,1)S(1)}, bf16[1,12,512,128]{3,2,1,0:T(8,128)(2,1)}, u32[]{:S(2)}) %copy-start.1) | copy-done | bytes 1572888
  4.2 0.0 copy-start.2
  4.2 0.7 %copy-done.2 = s32[27,3]{0,1:T(4,128)S(1)} copy-done((s32[27,3]{0,1:T(4,128)S(1)}, s32[27,3]{0,1:T(4,128)}, u32[]{:S(2)}) %copy-start.2) | copy-done | bytes 348
  4.9 0.0 copy-start.3
  4.9 0.7 %copy-done.3 = s32[8,2]{0,1:T(2,128)S(1)} copy-done((s32[8,2]{0,1:T(2,128)S(1)}, s32[8,2]{0,1:T(2,128)}, u32[]{:S(2)}) %copy-start.3) | copy-done | bytes 88
  5.6 40.5 %meson_fields.1 = (f32[7,8,128]{2,1,0:T(8,128)S(1)}, f32[8,128]{1,0:T(8,128)S(1)}) custom-call(s32[3,27]{1,0:T(4,128)S(1)} %bitcast.17, s32[2,8]{1,0:T(2,128)S(1)} %bitcast.19, s32[27,3]{1,0:T(8,128)S(1)} %copy.8.mom_v, s32[12,64,512]{2,1,0:T(8,128)S(1)} %bitcast.15, bf16[12,512,128]{2,1,0:T(8,128)(2,1)S(1)} %bitcast.16), custom_call_target="tpu_custom_call" | custom-call | tf_op jit(solution)/shard_map/meson_fields/pallas_call | solution.py:305
  46.1 0.1 reshape.16
  46.2 0.7 %copy.13 = f32[27,2,2,64]{3,1,0,2:T(2,128)} copy(f32[27,2,2,64]{3,2,1,0:T(2,128)S(1)} %slice.12) | data formatting | bytes 55296
  46.9 0.1 reshape.18
  46.9 0.2 copy.10
  47.1 0.7 %reshape.19 = f32[8,2,28]{2,1,0:T(2,128)} reshape(f32[16,7,4]{2,1,0:T(8,128)S(1)} %copy.10) | data formatting | bytes 3584 | tf_op jit(solution)/shard_map/reshape | solution.py:347
  (2 shorter events, 0.0 us)
Async XLA Ops:
  1.4 1.4 %copy-start = (s32[1,64,12,512]{3,1,2,0:T(8,128)S(1)}, s32[1,64,12,512]{3,1,2,0:T(8,128)}, u32[]{:S(2)}) copy-start(s32[1,64,12,512]{3,1,2,0:T(8,128)} %param.5) | copy-start | bytes 4718596
  2.8 1.4 %copy-start.1 = (bf16[1,12,512,128]{3,2,1,0:T(8,128)(2,1)S(1)}, bf16[1,12,512,128]{3,2,1,0:T(8,128)(2,1)}, u32[]{:S(2)}) copy-start(bf16[1,12,512,128]{3,2,1,0:T(8,128)(2,1)} %param.4) | copy-start | bytes 4718596
  4.2 0.7 %copy-start.2 = (s32[27,3]{0,1:T(4,128)S(1)}, s32[27,3]{0,1:T(4,128)}, u32[]{:S(2)}) copy-start(s32[27,3]{0,1:T(4,128)} %param.6) | copy-start | bytes 976
  4.9 0.7 %copy-start.3 = (s32[8,2]{0,1:T(2,128)S(1)}, s32[8,2]{0,1:T(2,128)}, u32[]{:S(2)}) copy-start(s32[8,2]{0,1:T(2,128)} %param.7) | copy-start | bytes 196

commit v3 on v2

v3 whole, which is shorter than its diff:
```python
import math

import jax
import jax.numpy as jnp
from jax import lax
from jax.experimental import pallas as pl
from jax.experimental.pallas import tpu as pltpu
from jax.sharding import PartitionSpec as P

EXTENT = 48
MOMS = 27
CHUNKS = 7
SIZE1, SIZE2 = 1.625, 1.1325
MESH = pl.DeviceIdType.MESH
PLANE = [(e, d) for e in range(2) for d in range(8) if (e, d) != (0, 0)]


def iota(shape, dim):
    return lax.broadcasted_iota(jnp.int32, shape, dim)


def swap_halves(array):
    return jnp.concatenate([array[:, 64:], array[:, :64]], axis=1)


def swapped(low, high, bit):
    has_bit = (iota((8, 128), 0) & bit) != 0
    return (
        jnp.where(has_bit, pltpu.roll(high, bit, 0), low),
        jnp.where(has_bit, high, pltpu.roll(low, 8 - bit, 0)),
    )


def fields_kernel(
    mom_h, pair_h, noise_h, vec_h, mesons, traces,
    mom_s, pair_s, spread, noise_v, vec_v, lhs, rhs, hrow, kap_r, kap_i,
    sums, raw, core_in, own, z_in, mine, slices, here, turned, both, chips,
    small_sem, noise_sem, vec_sem, core_s, core_r, z_s, z_r, t_s, t_r, last_s, last_r,
):
    space, tm = lax.axis_index("space"), lax.axis_index("tm")
    z, y, core = space // 4, lax.rem(space // 2, 2), lax.rem(space, 2)
    quad = lax.rem(space, 4)

    def in_z(d):
        return {"space": lax.rem(z + d, 8) * 4 + quad, "tm": tm}

    def in_quad(d):
        return {"space": z * 4 + (quad ^ d), "tm": tm}

    def in_plane(e, d):
        return {"space": space ^ (2 * e), "tm": lax.rem(tm + d, 8)}

    def in_chips(e, d):
        return {"space": (lax.rem(z + d, 8) * 4 + quad) ^ (2 * e), "tm": tm}

    def load(tile):
        lanes = pl.ds(tile * 128, 128)
        return (
            pltpu.make_async_copy(noise_h.at[:, :, lanes], noise_v.at[tile], noise_sem.at[tile]),
            pltpu.make_async_copy(vec_h.at[:, lanes, :], vec_v.at[tile], vec_sem.at[tile]),
        )

    small = (
        pltpu.make_async_copy(mom_h, mom_s, small_sem.at[0]),
        pltpu.make_async_copy(pair_h, pair_s, small_sem.at[1]),
    )
    for copy in small:
        copy.start()
    for tile in range(4):
        for copy in load(tile):
            copy.start()

    barrier = pltpu.get_barrier_semaphore()
    pl.semaphore_signal(barrier, inc=1, device_id=in_quad(1), device_id_type=MESH)
    for e, d in PLANE:
        pl.semaphore_signal(barrier, inc=1, device_id=in_chips(e, d), device_id_type=MESH)
        if d > 0:
            pl.semaphore_signal(barrier, inc=1, device_id=in_plane(e, d), device_id_type=MESH)

    hrow[...] = jnp.zeros_like(hrow)
    for copy in small:
        copy.wait()
    for q in range(MOMS):
        for k in range(3):
            spread[k, q : q + 1, :] = jnp.full((1, 128), mom_s[k, q], jnp.int32)

    scale = 1.0 / math.sqrt(12 * 512 * 32)
    row = space * 512 // EXTENT + iota((MOMS, 128), 1)
    q0 = jnp.abs(spread[0])
    angle = (spread[1] * lax.rem(row, EXTENT) + spread[2] * (row // EXTENT)).astype(jnp.float32)
    angle = angle * jnp.float32(2.0 * math.pi / EXTENT)
    size = jnp.where(q0 == 0, scale, jnp.where(q0 == 1, scale / SIZE1, scale / SIZE2))
    phase_r, phase_i = jnp.cos(angle) * size, -jnp.sin(angle) * size
    left = iota((MOMS, 128), 1) < 64
    for r in range(12):
        kap_r[r] = jnp.broadcast_to(phase_r[:, r : r + 1], (MOMS, 128))
        column = jnp.broadcast_to(phase_i[:, r : r + 1], (MOMS, 128))
        kap_i[r] = jnp.where(left, column, -column)

    phase0 = lax.rem(space * 32, EXTENT)
    lane = lax.rem(iota((8, 128), 1), 64)
    kind = iota((8, 128), 0)
    harmonic = jnp.where(kind < 2, 1, 2)
    amplitude = jnp.where(kind < 2, SIZE1, SIZE2)
    negate = iota((16, 128), 1) < 64

    def tile_step(tile, _):
        for copy in load(tile):
            copy.wait()
        starts = [phase0 + tile * 128 + 64 * h for h in range(2)]
        firsts = [lax.rem(start, EXTENT) for start in starts]
        waves = []
        for first in firsts:
            turn = ((first + lane) * harmonic).astype(jnp.float32) * jnp.float32(2.0 * math.pi / EXTENT)
            waves.append((amplitude * jnp.where(kind % 2 == 0, jnp.cos(turn), jnp.sin(turn))).astype(jnp.bfloat16))
        for a4 in range(3):
            n = [noise_v[tile, 4 * a4 + a].astype(jnp.float32).astype(jnp.bfloat16) for a in range(4)]
            for h in range(2):
                cut = slice(64 * h, 64 * h + 64)
                for two in range(2):
                    both = jnp.concatenate([n[2 * two][:, cut], n[2 * two + 1][:, cut]], axis=1)
                    z4_r, z4_i = jnp.abs(both - 2) - 1, jnp.abs(both - 1) - 1
                    at = a4 * 512 + two * 128
                    for f in range(5):
                        rows = pl.ds(64 * f, 64)
                        if f == 0:
                            first_part, second_part = z4_r, z4_i
                        else:
                            wave = waves[h][f - 1 : f, :]
                            if f % 2 == 1:
                                first_part, second_part = z4_r * wave, z4_i * wave
                            else:
                                first_part, second_part = z4_i * (-wave), z4_r * wave
                        lhs[h, rows, at : at + 128] = first_part
                        lhs[h, rows, at + 256 : at + 384] = second_part
                for a in range(4):
                    for g in range(4):
                        v = vec_v[tile, 4 * a4 + a, 64 * h + 16 * g : 64 * h + 16 * g + 16, :]
                        t = swap_halves(v)
                        t = jnp.where(negate, -t, t)
                        in_first = firsts[h] + 16 * g < EXTENT
                        zero = jnp.zeros_like(v)
                        at = a4 * 512 + 64 * a + 16 * g
                        rhs[h, at : at + 16, 0:128] = jnp.where(in_first, v, zero)
                        rhs[h, at : at + 16, 128:256] = jnp.where(in_first, zero, v)
                        rhs[h, at + 256 : at + 272, 0:128] = jnp.where(in_first, t, zero)
                        rhs[h, at + 256 : at + 272, 128:256] = jnp.where(in_first, zero, t)
        for h in range(2):
            out = jnp.dot(lhs[h], rhs[h], preferred_element_type=jnp.float32)
            f = [out[64 * k : 64 * k + 64, :] for k in range(5)]
            terms = [f[3] + f[4], f[1] + f[2], f[0], f[1] - f[2], f[3] - f[4]]
            for k in range(5):
                for r in range(2):
                    hrow[k, starts[h] // EXTENT + r] += terms[k][:, 128 * r : 128 * r + 128]
        return 0

    lax.fori_loop(0, 4, tile_step, 0)
    pl.semaphore_wait(barrier, 30)

    def to_core(g):
        return pltpu.make_async_remote_copy(
            src_ref=raw.at[1 - core, g], dst_ref=core_in.at[g], send_sem=core_s.at[g], recv_sem=core_r.at[g],
            device_id=in_quad(1), device_id_type=MESH,
        )

    def to_z(g, d):
        return pltpu.make_async_remote_copy(
            src_ref=own.at[g, lax.rem(z + d, 8)], dst_ref=z_in.at[g, d - 1],
            send_sem=z_s.at[g, d - 1], recv_sem=z_r.at[g, d - 1], device_id=in_z(d), device_id_type=MESH,
        )

    def to_plane(g, e, d):
        return pltpu.make_async_remote_copy(
            src_ref=mine.at[g, y ^ e], dst_ref=slices.at[g, y, tm],
            send_sem=t_s.at[g, e, d], recv_sem=t_r.at[g, e, d], device_id=in_plane(e, d), device_id_type=MESH,
        )

    def momentum(g, k):
        q = lax.min(4 * g + k, MOMS - 1)
        q0 = mom_s[0, q] + 2
        acc_r = [jnp.zeros((8, 128), jnp.float32) for _ in range(8)]
        acc_i = [jnp.zeros((8, 128), jnp.float32) for _ in range(8)]
        for r in range(12):
            k_r = jnp.broadcast_to(kap_r[r, pl.ds(q, 1), :], (8, 128))
            k_i = jnp.broadcast_to(kap_i[r, pl.ds(q, 1), :], (8, 128))
            for i in range(8):
                part = hrow[q0, r, 8 * i : 8 * i + 8, :]
                acc_r[i] += k_r * part
                acc_i[i] += k_i * part
        for i in range(8):
            sums[k, i] = acc_r[i] + swap_halves(acc_i[i])

    def after_core(g):
        to_core(g).wait_recv()
        own[g] = raw[core, g] + core_in[g]
        for d in range(1, 8):
            to_z(g, d).start()

    def first_step(g, _):
        def one(k, _):
            momentum(g, k)
            return 0

        lax.fori_loop(0, 4, one, 0)
        for i in range(8):
            low = [swapped(sums[2 * k, i], sums[2 * k + 1, i], 2) for k in range(2)]
            for c in range(2):
                pair = swapped(low[0][c], low[1][c], 4)
                for yy in range(2):
                    raw[c, g, i, yy] = pair[yy]
        to_core(g).start()

        @pl.when(g >= 1)
        def _():
            after_core(g - 1)

        return 0

    lax.fori_loop(0, CHUNKS, first_step, 0)
    after_core(CHUNKS - 1)

    def after_z(g, _):
        total = own[g, z]
        for d in range(1, 8):
            to_z(g, d).wait_recv()
            total += z_in[g, d - 1]
        mine[g] = total
        slices[g, y, tm] = mine[g, y]
        for e, d in PLANE:
            to_plane(g, e, d).start()
        return 0

    lax.fori_loop(0, CHUNKS, after_z, 0)

    lanes = iota((8, 128), 1)

    def after_plane(g, result):
        for e, d in PLANE:
            to_plane(g, e, d).wait_recv()
        for t in range(8):
            tile = slices[g, 0, t] + slices[g, 1, t]
            here[t] = tile
            turned[t] = swap_halves(jnp.where(lanes < 64, tile, -tile))
        mesons[g] = slices[g, 0, tm] + slices[g, 1, tm]
        for k in range(8):
            sink, source, rotated = here[pair_s[1, k]], here[pair_s[0, k]], turned[pair_s[0, k]]
            for c, term in enumerate((sink * source, sink * rotated)):
                value = jnp.sum(term, axis=1, keepdims=True)
                result = jnp.where(lanes == (2 * k + c) * CHUNKS + g, value, result)
        return result

    result = lax.fori_loop(0, CHUNKS, after_plane, jnp.zeros((8, 128), jnp.float32))
    result = result + pltpu.roll(result, 7, 0)
    for k in range(4):
        both[core, k : k + 1, :] = result[2 * k : 2 * k + 1, :]

    to_other = pltpu.make_async_remote_copy(
        src_ref=both.at[core], dst_ref=both.at[core], send_sem=last_s.at[0], recv_sem=last_r.at[0],
        device_id=in_quad(1), device_id_type=MESH,
    )
    chip = z * 2 + y

    def to_chip(e, d):
        return pltpu.make_async_remote_copy(
            src_ref=chips.at[chip], dst_ref=chips.at[chip], send_sem=last_s.at[8 * e + d], recv_sem=last_r.at[8 * e + d],
            device_id=in_chips(e, d), device_id_type=MESH,
        )

    to_other.start()
    to_other.wait_recv()
    chips[chip] = both[0] + both[1]
    for e, d in PLANE:
        to_chip(e, d).start()
    for e, d in PLANE:
        to_chip(e, d).wait_recv()
    total = chips[0]
    for k in range(1, 16):
        total += chips[k]
    traces[...] = total * (1.0 / 64)

    def finish(g, _):
        to_core(g).wait_send()
        for d in range(1, 8):
            to_z(g, d).wait_send()
        for e, d in PLANE:
            to_plane(g, e, d).wait_send()
        return 0

    lax.fori_loop(0, CHUNKS, finish, 0)
    to_other.wait_send()
    for e, d in PLANE:
        to_chip(e, d).wait_send()


def local(solutions, noise, momenta, pairs):
    f32, bf16 = jnp.float32, jnp.bfloat16
    vmem = pl.BlockSpec(memory_space=pltpu.VMEM)
    hbm = pl.BlockSpec(memory_space=pltpu.HBM)
    dma = pltpu.SemaphoreType.DMA
    mesons, traces = pl.pallas_call(
        fields_kernel,
        out_shape=(
            jax.ShapeDtypeStruct((CHUNKS, 8, 128), f32),
            jax.ShapeDtypeStruct((4, 128), f32),
        ),
        in_specs=[hbm] * 4,
        out_specs=(vmem, vmem),
        scratch_shapes=[
            pltpu.SMEM((3, MOMS), jnp.int32),
            pltpu.SMEM((2, 8), jnp.int32),
            pltpu.VMEM((3, MOMS, 128), jnp.int32),
            pltpu.VMEM((4, 12, 64, 128), jnp.int32),
            pltpu.VMEM((4, 12, 128, 128), bf16),
            pltpu.VMEM((2, 320, 1536), bf16),
            pltpu.VMEM((2, 1536, 256), bf16),
            pltpu.VMEM((5, 12, 64, 128), f32),
            pltpu.VMEM((12, MOMS, 128), f32),
            pltpu.VMEM((12, MOMS, 128), f32),
            pltpu.VMEM((4, 8, 8, 128), f32),
            pltpu.VMEM((2, CHUNKS, 8, 2, 8, 128), f32),
            pltpu.VMEM((CHUNKS, 8, 2, 8, 128), f32),
            pltpu.VMEM((CHUNKS, 8, 2, 8, 128), f32),
            pltpu.VMEM((CHUNKS, 7, 2, 8, 128), f32),
            pltpu.VMEM((CHUNKS, 2, 8, 128), f32),
            pltpu.VMEM((CHUNKS, 2, 8, 8, 128), f32),
            pltpu.VMEM((8, 8, 128), f32),
            pltpu.VMEM((8, 8, 128), f32),
            pltpu.VMEM((2, 4, 128), f32),
            pltpu.VMEM((16, 4, 128), f32),
            dma((2,)), dma((4,)), dma((4,)),
            dma((CHUNKS,)), dma((CHUNKS,)),
            dma((CHUNKS, 7)), dma((CHUNKS, 7)),
            dma((CHUNKS, 2, 8)), dma((CHUNKS, 2, 8)),
            dma((16,)), dma((16,)),
        ],
        compiler_params=pltpu.CompilerParams(
            collective_id=0, has_side_effects=True, vmem_limit_bytes=67043328
        ),
        name="meson_fields",
    )(momenta.T, pairs.T, noise[0].transpose(1, 0, 2), solutions[0])
    mesons = mesons.reshape(4 * CHUNKS, 2, 2, 64)[:MOMS].transpose(2, 0, 1, 3)[None]
    traces = traces[:, : 16 * CHUNKS].reshape(4, 16, CHUNKS)
    correlators = traces.transpose(1, 2, 0).reshape(8, 2, 4 * CHUNKS)[:, :, :MOMS]
    return (mesons, correlators)


def solution(mesh):
    in_specs = (P("tm", None, "space", None), P("tm", None, None, "space"), P(), P("tm", None))
    out_specs = (P("tm", None, None, "space", None), P("tm", None, None))
    return jax.shard_map(local, mesh=mesh, in_specs=in_specs, out_specs=out_specs, check_vma=False)
```

time: 48 us -> 46.6 us (0.971)
  local copies, waits for them, and re-layouts: 6.68 us -> 3.14 us
  Pallas kernels: 40.5 us -> 42.6 us
    unnamed x10 -> x1, local copies, waits for them, and re-layouts: 5.6 us -> 0.65 us
    pallas_call x1, Pallas kernels: 40.5 us -> 42.6 us  [local(): pl.pallas_call(fields_kernel, out_shape=(jax.ShapeDtypeStruct((CHUNKS, 8,...]
    reshape x1, local copies, waits for them, and re-layouts: 0.09 us -> 0.84 us  [local(): mesons.reshape(4 * CHUNKS, 2, 2, 64)[:MOMS].transpose(2, 0, 1, 3)[None]]
    reshape x1, local copies, waits for them, and re-layouts: 0.08 us -> 0.75 us  [local(): traces = traces[:, :16 * CHUNKS].reshape(4, 16, CHUNKS)]
where the time goes in v3:
time: 46.6 us; the launch traced here: 46.4 us
  Pallas kernels  42.6 us (91%)
  local copies, waits for them, and re-layouts  3.14 us (7%)
  between operations  0.66 us (1%)
    pallas_call x1, Pallas kernels, local(): pl.pallas_call(fields_kernel, out_shape=(jax.ShapeDtypeStruct((CHUNKS, 8,...  42.6 us

profile of v3, /device:TPU:1, one launch (start us, length us, event | category | flops | bytes accessed | tf_op | source)
XLA Modules:
  0.0 46.4 jit_solution(4851119376740557885)
XLA Ops:
  0.6 42.6 %meson_fields.1 = (f32[7,8,128]{2,1,0:T(8,128)}, f32[4,128]{1,0:T(4,128)}) custom-call(s32[3,27]{1,0:T(4,128)} %bitcast.19, s32[2,8]{1,0:T(2,128)} %bitcast.21, s32[12,64,512]{2,1,0:T(8,128)} %bitcast.14, bf16[12,512,128]{2,1,0:T(8,128)(2,1)} %bitcast.15), custom_call_target="tpu_custom_call" | custom-call | tf_op jit(solution)/shard_map/meson_fields/pallas_call | solution.py:300
  43.2 0.8 %reshape.13 = f32[28,2,2,64]{3,2,1,0:T(2,128)S(1)} reshape(f32[7,8,128]{2,1,0:T(8,128)} %get-tuple-element.4) | data formatting | bytes 57344 | tf_op jit(solution)/shard_map/reshape | solution.py:341
  44.1 0.7 %copy.12 = f32[27,2,2,64]{3,1,0,2:T(2,128)} copy(f32[27,2,2,64]{3,2,1,0:T(2,128)S(1)} %slice.12) | data formatting | bytes 55296
  44.8 0.7 %reshape.14 = f32[4,16,7]{2,1,0:T(8,128)S(1)} reshape(f32[4,112]{1,0:T(4,128)} %bitcast.20) | data formatting | bytes 3584 | tf_op jit(solution)/shard_map/reshape | solution.py:342
  45.5 0.2 copy.9
  45.7 0.7 %reshape.15 = f32[8,2,28]{2,1,0:T(2,128)} reshape(f32[16,7,4]{2,1,0:T(8,128)S(1)} %copy.9) | data formatting | bytes 3584 | tf_op jit(solution)/shard_map/reshape | solution.py:343
  (1 shorter events, 0.0 us)

commit v4 on v2

--- a/solution.py
+++ b/solution.py
@@ -31,10 +31,10 @@
 
 
 def fields_kernel(
-    mom_s, pair_s, mom_v, noise_h, vec_h, mesons, traces,
-    noise_v, vec_v, lhs, rhs, hrow, kap_r, kap_i,
+    mom_h, pair_h, noise_h, vec_h, mesons, traces,
+    mom_s, pair_s, spread, noise_v, vec_v, hrow, kap_r, kap_i,
     raw, core_in, half, y_in, own, z_in, slices, here, turned, four, eight,
-    noise_sem, vec_sem, core_s, core_r, y_s, y_r, z_s, z_r, t_s, t_r, four_s, four_r, eight_s, eight_r,
+    small_sem, noise_sem, vec_sem, core_s, core_r, y_s, y_r, z_s, z_r, t_s, t_r, four_s, four_r, eight_s, eight_r,
 ):
     space, tm = lax.axis_index("space"), lax.axis_index("tm")
     z, y, core = space // 4, lax.rem(space // 2, 2), lax.rem(space, 2)
@@ -56,6 +56,12 @@
             pltpu.make_async_copy(vec_h.at[:, lanes, :], vec_v.at[tile], vec_sem.at[tile]),
         )
 
+    small = (
+        pltpu.make_async_copy(mom_h, mom_s, small_sem.at[0]),
+        pltpu.make_async_copy(pair_h, pair_s, small_sem.at[1]),
+    )
+    for copy in small:
+        copy.start()
     for tile in range(4):
         for copy in load(tile):
             copy.start()
@@ -67,10 +73,19 @@
         pl.semaphore_signal(barrier, inc=1, device_id=in_z(d), device_id_type=MESH)
         pl.semaphore_signal(barrier, inc=1, device_id=in_tm(d), device_id_type=MESH)
 
+    for k in range(5):
+        hrow[k, 0] = jnp.zeros((64, 128), jnp.float32)
+        hrow[k, 11] = jnp.zeros((64, 128), jnp.float32)
+    for copy in small:
+        copy.wait()
+    for q in range(MOMS):
+        for k in range(3):
+            spread[k, q : q + 1, :] = jnp.full((1, 128), mom_s[k, q], jnp.int32)
+
     scale = 1.0 / math.sqrt(12 * 512 * 32)
     row = space * 512 // EXTENT + iota((MOMS, 128), 1)
-    q0 = jnp.abs(mom_v[:, 0:1])
-    angle = (mom_v[:, 1:2] * lax.rem(row, EXTENT) + mom_v[:, 2:3] * (row // EXTENT)).astype(jnp.float32)
+    q0 = jnp.abs(spread[0])
+    angle = (spread[1] * lax.rem(row, EXTENT) + spread[2] * (row // EXTENT)).astype(jnp.float32)
     angle = angle * jnp.float32(2.0 * math.pi / EXTENT)
     size = jnp.where(q0 == 0, scale, jnp.where(q0 == 1, scale / SIZE1, scale / SIZE2))
     phase_r, phase_i = jnp.cos(angle) * size, -jnp.sin(angle) * size
@@ -80,13 +95,12 @@
         column = jnp.broadcast_to(phase_i[:, r : r + 1], (MOMS, 128))
         kap_i[r] = jnp.where(left, column, -column)
 
-    hrow[...] = jnp.zeros_like(hrow)
     phase0 = lax.rem(space * 32, EXTENT)
     lane = lax.rem(iota((8, 128), 1), 64)
     kind = iota((8, 128), 0)
     harmonic = jnp.where(kind < 2, 1, 2)
     amplitude = jnp.where(kind < 2, SIZE1, SIZE2)
-    negate = iota((16, 128), 1) < 64
+    flip = jnp.where(iota((64, 128), 1) < 64, -1.0, 1.0).astype(jnp.bfloat16)
 
     def tile_step(tile, _):
         for copy in load(tile):
@@ -96,46 +110,48 @@
         waves = []
         for first in firsts:
             turn = ((first + lane) * harmonic).astype(jnp.float32) * jnp.float32(2.0 * math.pi / EXTENT)
-            waves.append((amplitude * jnp.where(kind % 2 == 0, jnp.cos(turn), jnp.sin(turn))).astype(jnp.bfloat16))
+            wave = amplitude * jnp.where(kind % 2 == 0, jnp.cos(turn), jnp.sin(turn))
+            waves.append(wave.astype(jnp.bfloat16))
+        totals = [None, None]
         for a4 in range(3):
             n = [noise_v[tile, 4 * a4 + a].astype(jnp.float32).astype(jnp.bfloat16) for a in range(4)]
             for h in range(2):
                 cut = slice(64 * h, 64 * h + 64)
-                for two in range(2):
-                    both = jnp.concatenate([n[2 * two][:, cut], n[2 * two + 1][:, cut]], axis=1)
-                    z4_r, z4_i = jnp.abs(both - 2) - 1, jnp.abs(both - 1) - 1
-                    at = a4 * 512 + two * 128
-                    for f in range(5):
-                        rows = pl.ds(64 * f, 64)
-                        if f == 0:
-                            first_part, second_part = z4_r, z4_i
-                        else:
-                            wave = waves[h][f - 1 : f, :]
-                            if f % 2 == 1:
-                                first_part, second_part = z4_r * wave, z4_i * wave
+                joined = [jnp.concatenate([n[k][:, cut], n[k + 1][:, cut]], axis=1) for k in (0, 2)]
+                n4 = jnp.concatenate(joined, axis=1)
+                z4_r, z4_i = jnp.abs(n4 - 2) - 1, jnp.abs(n4 - 1) - 1
+                wave = [jnp.concatenate([waves[h][k : k + 1, :]] * 2, axis=1) for k in range(4)]
+                left_r = [z4_r, z4_r * wave[0], z4_i * -wave[1], z4_r * wave[2], z4_i * -wave[3]]
+                left_i = [z4_i, z4_i * wave[0], z4_r * wave[1], z4_i * wave[2], z4_r * wave[3]]
+                right_r, right_i = [], []
+                for a in range(4):
+                    v = vec_v[tile, 4 * a4 + a, 64 * h : 64 * h + 64, :]
+                    t = swap_halves(v) * flip
+                    for part, into in ((v, right_r), (t, right_i)):
+                        for g in range(4):
+                            piece = part[16 * g : 16 * g + 16]
+                            zero = jnp.zeros_like(piece)
+                            if g == 0:
+                                pair = [piece, zero]
+                            elif g == 3:
+                                pair = [zero, piece]
                             else:
-                                first_part, second_part = z4_i * (-wave), z4_r * wave
-                        lhs[h, rows, at : at + 128] = first_part
-                        lhs[h, rows, at + 256 : at + 384] = second_part
-                for a in range(4):
-                    for g in range(4):
-                        v = vec_v[tile, 4 * a4 + a, 64 * h + 16 * g : 64 * h + 16 * g + 16, :]
-                        t = swap_halves(v)
-                        t = jnp.where(negate, -t, t)
-                        in_first = firsts[h] + 16 * g < EXTENT
-                        zero = jnp.zeros_like(v)
-                        at = a4 * 512 + 64 * a + 16 * g
-                        rhs[h, at : at + 16, 0:128] = jnp.where(in_first, v, zero)
-                        rhs[h, at : at + 16, 128:256] = jnp.where(in_first, zero, v)
-                        rhs[h, at + 256 : at + 272, 0:128] = jnp.where(in_first, t, zero)
-                        rhs[h, at + 256 : at + 272, 128:256] = jnp.where(in_first, zero, t)
+                                in_first = firsts[h] + 16 * g < EXTENT
+                                pair = [jnp.where(in_first, piece, zero), jnp.where(in_first, zero, piece)]
+                            into.append(jnp.concatenate(pair, axis=1))
+                for lhs, rhs in ((left_r, right_r), (left_i, right_i)):
+                    product = jnp.dot(
+                        jnp.concatenate(lhs, axis=0), jnp.concatenate(rhs, axis=0), preferred_element_type=jnp.float32
+                    )
+                    totals[h] = product if totals[h] is None else totals[h] + product
         for h in range(2):
-            out = jnp.dot(lhs[h], rhs[h], preferred_element_type=jnp.float32)
-            f = [out[64 * k : 64 * k + 64, :] for k in range(5)]
+            f = [totals[h][64 * k : 64 * k + 64, :] for k in range(5)]
             terms = [f[3] + f[4], f[1] + f[2], f[0], f[1] - f[2], f[3] - f[4]]
+            fresh = firsts[h] == 0 if h == 1 else (firsts[h] == 0) | (tile == 0)
             for k in range(5):
-                for r in range(2):
-                    hrow[k, starts[h] // EXTENT + r] += terms[k][:, 128 * r : 128 * r + 128]
+                at = starts[h] // EXTENT
+                hrow[k, at] = jnp.where(fresh, 0.0, hrow[k, at]) + terms[k][:, 0:128]
+                hrow[k, at + 1] = terms[k][:, 128:256]
         return 0
 
     lax.fori_loop(0, 4, tile_step, 0)
@@ -192,11 +208,8 @@
         to_y(g).start()
 
     def first_step(g, _):
-        def one(k, _):
+        for k in range(4):
             momentum(g, k)
-            return 0
-
-        lax.fori_loop(0, 4, one, 0)
         to_core(g).start()
 
         @pl.when(g >= 1)
@@ -229,7 +242,9 @@
         for d in range(1, 8):
             to_z(g, d).wait_recv()
             total += z_in[g, d - 1]
-        mesons[g] = total
+        for k in range(4):
+            for c in range(2):
+                mesons[c, 4 * g + k] = total[2 * k : 2 * k + 2, 64 * c : 64 * c + 64]
         slices[g, tm] = total
         for d in range(1, 8):
             to_tm(g, d).start()
@@ -250,10 +265,13 @@
             sink, source, rotated = here[pair_s[1, k]], here[pair_s[0, k]], turned[pair_s[0, k]]
             for c, term in enumerate((sink * source, sink * rotated)):
                 value = jnp.sum(term, axis=1, keepdims=True)
-                sums = jnp.where(lanes == (2 * k + c) * CHUNKS + g, value, sums)
+                sums = jnp.where(lanes == 16 * g + 2 * k + c, value, sums)
         return sums
 
-    four[quad] = lax.fori_loop(0, CHUNKS, after_tm, jnp.zeros((8, 128), jnp.float32))
+    result = lax.fori_loop(0, CHUNKS, after_tm, jnp.zeros((8, 128), jnp.float32))
+    result = result + pltpu.roll(result, 7, 0)
+    for k in range(4):
+        four[quad, k : k + 1, :] = result[2 * k : 2 * k + 1, :]
 
     def to_quad(d):
         return pltpu.make_async_remote_copy(
@@ -279,7 +297,10 @@
     total = eight[0]
     for k in range(1, 8):
         total += eight[k]
-    traces[...] = total * (1.0 / 64)
+    columns = jnp.transpose(jnp.concatenate([total, total], axis=0) * (1.0 / 64))
+    by_moment = jnp.concatenate([columns[16 * g : 16 * g + 16, 0:4] for g in range(CHUNKS)], axis=1)
+    for k in range(8):
+        traces[k] = by_moment[2 * k : 2 * k + 2, 0:MOMS]
 
     def finish(g, _):
         to_core(g).wait_send()
@@ -296,25 +317,36 @@
         to_all_z(d).wait_send()
 
 
+def write_kernel(mesons_v, traces_v, mesons_h, traces_h, sem):
+    copies = (
+        pltpu.make_async_copy(mesons_v.at[:, pl.ds(0, MOMS)], mesons_h, sem.at[0]),
+        pltpu.make_async_copy(traces_v, traces_h, sem.at[1]),
+    )
+    for copy in copies:
+        copy.start()
+    for copy in copies:
+        copy.wait()
+
+
 def local(solutions, noise, momenta, pairs):
     f32, bf16 = jnp.float32, jnp.bfloat16
     vmem = pl.BlockSpec(memory_space=pltpu.VMEM)
-    smem = pl.BlockSpec(memory_space=pltpu.SMEM)
-    hbm = pl.BlockSpec(memory_space=pl.ANY)
+    hbm = pl.BlockSpec(memory_space=pltpu.HBM)
     dma = pltpu.SemaphoreType.DMA
     mesons, traces = pl.pallas_call(
         fields_kernel,
         out_shape=(
-            jax.ShapeDtypeStruct((CHUNKS, 8, 128), f32),
-            jax.ShapeDtypeStruct((8, 128), f32),
+            pltpu.VMEM((2, 4 * CHUNKS, 2, 64), f32),
+            pltpu.VMEM((8, 2, MOMS), f32),
         ),
-        in_specs=[smem, smem, vmem, hbm, hbm],
+        in_specs=[hbm] * 4,
         out_specs=(vmem, vmem),
         scratch_shapes=[
+            pltpu.SMEM((3, MOMS), jnp.int32),
+            pltpu.SMEM((2, 8), jnp.int32),
+            pltpu.VMEM((3, MOMS, 128), jnp.int32),
             pltpu.VMEM((4, 12, 64, 128), jnp.int32),
             pltpu.VMEM((4, 12, 128, 128), bf16),
-            pltpu.VMEM((2, 320, 1536), bf16),
-            pltpu.VMEM((2, 1536, 256), bf16),
             pltpu.VMEM((5, 12, 64, 128), f32),
             pltpu.VMEM((12, MOMS, 128), f32),
             pltpu.VMEM((12, MOMS, 128), f32),
@@ -327,9 +359,9 @@
             pltpu.VMEM((CHUNKS, 8, 8, 128), f32),
             pltpu.VMEM((8, 8, 128), f32),
             pltpu.VMEM((8, 8, 128), f32),
-            pltpu.VMEM((4, 8, 128), f32),
-            pltpu.VMEM((8, 8, 128), f32),
-            dma((4,)), dma((4,)),
+            pltpu.VMEM((4, 4, 128), f32),
+            pltpu.VMEM((8, 4, 128), f32),
+            dma((2,)), dma((4,)), dma((4,)),
             dma((CHUNKS,)), dma((CHUNKS,)),
             dma((CHUNKS,)), dma((CHUNKS,)),
             dma((CHUNKS, 7)), dma((CHUNKS, 7)),
@@ -338,14 +370,23 @@
             dma((7,)), dma((7,)),
         ],
         compiler_params=pltpu.CompilerParams(
-            collective_id=0, has_side_effects=True, vmem_limit_bytes=40 * 1024 * 1024
+            collective_id=0, has_side_effects=True, vmem_limit_bytes=66700000
         ),
         name="meson_fields",
-    )(momenta.T, pairs.T, momenta, noise[0].transpose(1, 0, 2), solutions[0])
-    mesons = mesons.reshape(4 * CHUNKS, 2, 2, 64)[:MOMS].transpose(2, 0, 1, 3)[None]
-    traces = traces.reshape(4, 2, 128).sum(axis=1)[:, : 16 * CHUNKS].reshape(4, 16, CHUNKS)
-    correlators = traces.transpose(1, 2, 0).reshape(8, 2, 4 * CHUNKS)[:, :, :MOMS]
-    return (mesons, correlators)
+    )(momenta.T, pairs.T, noise[0].transpose(1, 0, 2), solutions[0])
+    mesons, correlators = pl.pallas_call(
+        write_kernel,
+        out_shape=(
+            jax.ShapeDtypeStruct((2, MOMS, 2, 64), f32),
+            jax.ShapeDtypeStruct((8, 2, MOMS), f32),
+        ),
+        in_specs=[vmem] * 2,
+        out_specs=(hbm, hbm),
+        scratch_shapes=[dma((2,))],
+        compiler_params=pltpu.CompilerParams(vmem_limit_bytes=1 << 20),
+        name="write_out",
+    )(mesons, traces)
+    return (mesons[None], correlators)
 
 
 def solution(mesh):

time: 48 us -> 40.2 us (0.84)
  local copies, waits for them, and re-layouts: 6.68 us -> 0 us
  Pallas kernels: 40.5 us -> 39.5 us
    unnamed x10 -> x0, local copies, waits for them, and re-layouts: 5.6 us -> none
    pallas_call x1 -> x2, Pallas kernels: 40.5 us -> 39.5 us  [the longest x1 38.9 us: local(): pl.pallas_call(fields_kernel, out_shape=(pltpu.VMEM((2, 4 * CHUNKS, 2, 64...]
    reshape x3 -> x0, local copies, waits for them, and re-layouts: 0.87 us -> none  [the longest x1 0.69 us: local(): traces.transpose(1, 2, 0).reshape(8, 2, 4 * CHUNKS)[:, :, :MOMS]]
where the time goes in v4:
time: 40.2 us; the launch traced here: 40.1 us
  Pallas kernels  39.5 us (98%)
  between operations  0.64 us (2%)
    pallas_call x1, Pallas kernels, local(): pl.pallas_call(fields_kernel, out_shape=(pltpu.VMEM((2, 4 * CHUNKS, 2, 64...  38.9 us

profile of v4, /device:TPU:1, one launch (start us, length us, event | category | flops | bytes accessed | tf_op | source)
XLA Modules:
  0.0 40.1 jit_solution(18022988163375000336)
XLA Ops:
  0.6 38.9 %meson_fields.1 = (f32[2,28,2,64]{3,2,1,0:T(2,128)S(1)}, f32[8,2,27]{2,1,0:T(2,128)S(1)}) custom-call(s32[3,27]{1,0:T(4,128)} %bitcast.9, s32[2,8]{1,0:T(2,128)} %bitcast.10, s32[12,64,512]{2,1,0:T(8,128)} %bitcast.7, bf16[12,512,128]{2,1,0:T(8,128)(2,1)} %bitcast.8), custom_call_target="tpu_custom_call" | custom-call | tf_op jit(solution)/shard_map/meson_fields/pallas_call | solution.py:336
  39.5 0.6 %write_out.1 = (f32[2,27,2,64]{3,2,1,0:T(2,128)}, f32[8,2,27]{2,1,0:T(2,128)}) custom-call(f32[2,28,2,64]{3,2,1,0:T(2,128)S(1)} %get-tuple-element.6.mesons_v, f32[8,2,27]{2,1,0:T(2,128)S(1)} %get-tuple-element.7.traces_v), custom_call_target="tpu_custom_call" | custom-call | tf_op jit(solution)/shard_map/write_out/pallas_call | solution.py:377

commit v5 on v4

--- a/solution.py
+++ b/solution.py
@@ -33,8 +33,8 @@
 def fields_kernel(
     mom_h, pair_h, noise_h, vec_h, mesons, traces,
     mom_s, pair_s, spread, noise_v, vec_v, hrow, kap_r, kap_i,
-    raw, core_in, half, y_in, own, z_in, slices, here, turned, four, eight,
-    small_sem, noise_sem, vec_sem, core_s, core_r, y_s, y_r, z_s, z_r, t_s, t_r, four_s, four_r, eight_s, eight_r,
+    raw, core_in, half, y_in, own, z_in, slices, here, turned, both, chips,
+    small_sem, noise_sem, vec_sem, core_s, core_r, y_s, y_r, z_s, z_r, t_s, t_r, last_s, last_r,
 ):
     space, tm = lax.axis_index("space"), lax.axis_index("tm")
     z, y, core = space // 4, lax.rem(space // 2, 2), lax.rem(space, 2)
@@ -45,6 +45,9 @@
 
     def in_quad(d):
         return {"space": z * 4 + (quad ^ d), "tm": tm}
+
+    def in_chips(e, d):
+        return {"space": (lax.rem(z + d, 8) * 4 + quad) ^ (2 * e), "tm": tm}
 
     def in_tm(d):
         return {"space": space, "tm": lax.rem(tm + d, 8)}
@@ -67,7 +70,7 @@
             copy.start()
 
     barrier = pltpu.get_barrier_semaphore()
-    for d in range(1, 4):
+    for d in range(1, 3):
         pl.semaphore_signal(barrier, inc=1, device_id=in_quad(d), device_id_type=MESH)
     for d in range(1, 8):
         pl.semaphore_signal(barrier, inc=1, device_id=in_z(d), device_id_type=MESH)
@@ -155,31 +158,34 @@
         return 0
 
     lax.fori_loop(0, 4, tile_step, 0)
-    pl.semaphore_wait(barrier, 17)
+    pl.semaphore_wait(barrier, 16)
 
     def to_core(g):
         return pltpu.make_async_remote_copy(
-            src_ref=raw.at[1 - core, g], dst_ref=core_in.at[g], send_sem=core_s.at[g], recv_sem=core_r.at[g],
+            src_ref=raw.at[1 - core, g], dst_ref=core_in.at[g], send_sem=core_s.at[0], recv_sem=core_r.at[g],
             device_id=in_quad(1), device_id_type=MESH,
         )
 
     def to_y(g):
         return pltpu.make_async_remote_copy(
-            src_ref=half.at[g, 1 - y], dst_ref=y_in.at[g], send_sem=y_s.at[g], recv_sem=y_r.at[g],
+            src_ref=half.at[g, 1 - y], dst_ref=y_in.at[g], send_sem=y_s.at[0], recv_sem=y_r.at[g],
             device_id=in_quad(2), device_id_type=MESH,
         )
 
     def to_z(g, d):
         return pltpu.make_async_remote_copy(
             src_ref=own.at[g, lax.rem(z + d, 8)], dst_ref=z_in.at[g, d - 1],
-            send_sem=z_s.at[g, d - 1], recv_sem=z_r.at[g, d - 1], device_id=in_z(d), device_id_type=MESH,
+            send_sem=z_s.at[0], recv_sem=z_r.at[g], device_id=in_z(d), device_id_type=MESH,
         )
 
     def to_tm(g, d):
         return pltpu.make_async_remote_copy(
             src_ref=slices.at[g, tm], dst_ref=slices.at[g, tm],
-            send_sem=t_s.at[g, d - 1], recv_sem=t_r.at[g, d - 1], device_id=in_tm(d), device_id_type=MESH,
-        )
+            send_sem=t_s.at[0], recv_sem=t_r.at[g], device_id=in_tm(d), device_id_type=MESH,
+        )
+
+    def arrive(ref, sem):
+        pltpu.make_async_copy(ref, ref, sem).wait()
 
     def momentum(g, k):
         q = lax.min(4 * g + k, MOMS - 1)
@@ -238,10 +244,10 @@
     lax.fori_loop(0, CHUNKS, after_y, 0)
 
     def after_z(g, _):
+        arrive(z_in.at[g], z_r.at[g])
         total = own[g, z]
-        for d in range(1, 8):
-            to_z(g, d).wait_recv()
-            total += z_in[g, d - 1]
+        for d in range(7):
+            total += z_in[g, d]
         for k in range(4):
             for c in range(2):
                 mesons[c, 4 * g + k] = total[2 * k : 2 * k + 2, 64 * c : 64 * c + 64]
@@ -255,8 +261,7 @@
     lanes = iota((8, 128), 1)
 
     def after_tm(g, sums):
-        for d in range(1, 8):
-            to_tm(g, d).wait_recv()
+        arrive(slices.at[g, pl.ds(0, 7)], t_r.at[g])
         for t in range(8):
             tile = slices[g, t]
             here[t] = tile
@@ -271,50 +276,40 @@
     result = lax.fori_loop(0, CHUNKS, after_tm, jnp.zeros((8, 128), jnp.float32))
     result = result + pltpu.roll(result, 7, 0)
     for k in range(4):
-        four[quad, k : k + 1, :] = result[2 * k : 2 * k + 1, :]
-
-    def to_quad(d):
-        return pltpu.make_async_remote_copy(
-            src_ref=four.at[quad], dst_ref=four.at[quad], send_sem=four_s.at[d - 1], recv_sem=four_r.at[d - 1],
-            device_id=in_quad(d), device_id_type=MESH,
-        )
-
-    def to_all_z(d):
-        return pltpu.make_async_remote_copy(
-            src_ref=eight.at[z], dst_ref=eight.at[z], send_sem=eight_s.at[d - 1], recv_sem=eight_r.at[d - 1],
-            device_id=in_z(d), device_id_type=MESH,
-        )
-
-    for d in range(1, 4):
-        to_quad(d).start()
-    for d in range(1, 4):
-        to_quad(d).wait_recv()
-    eight[z] = (four[0] + four[1]) + (four[2] + four[3])
-    for d in range(1, 8):
-        to_all_z(d).start()
-    for d in range(1, 8):
-        to_all_z(d).wait_recv()
-    total = eight[0]
-    for k in range(1, 8):
-        total += eight[k]
+        both[core, k : k + 1, :] = result[2 * k : 2 * k + 1, :]
+    to_other = pltpu.make_async_remote_copy(
+        src_ref=both.at[core], dst_ref=both.at[core], send_sem=last_s.at[0], recv_sem=last_r.at[0],
+        device_id=in_quad(1), device_id_type=MESH,
+    )
+    chip = z * 2 + y
+
+    def to_chip(e, d):
+        return pltpu.make_async_remote_copy(
+            src_ref=chips.at[chip], dst_ref=chips.at[chip], send_sem=last_s.at[1], recv_sem=last_r.at[1],
+            device_id=in_chips(e, d), device_id_type=MESH,
+        )
+
+    to_other.start()
+    to_other.wait_recv()
+    chips[chip] = both[0] + both[1]
+    for e in range(2):
+        for d in range(1 - e, 8):
+            to_chip(e, d).start()
+    arrive(chips.at[pl.ds(0, 15)], last_r.at[1])
+    total = chips[0]
+    for k in range(1, 16):
+        total += chips[k]
     columns = jnp.transpose(jnp.concatenate([total, total], axis=0) * (1.0 / 64))
     by_moment = jnp.concatenate([columns[16 * g : 16 * g + 16, 0:4] for g in range(CHUNKS)], axis=1)
     for k in range(8):
         traces[k] = by_moment[2 * k : 2 * k + 2, 0:MOMS]
 
-    def finish(g, _):
-        to_core(g).wait_send()
-        to_y(g).wait_send()
-        for d in range(1, 8):
-            to_z(g, d).wait_send()
-            to_tm(g, d).wait_send()
-        return 0
-
-    lax.fori_loop(0, CHUNKS, finish, 0)
-    for d in range(1, 4):
-        to_quad(d).wait_send()
-    for d in range(1, 8):
-        to_all_z(d).wait_send()
+    arrive(raw.at[0], core_s.at[0])
+    arrive(y_in, y_s.at[0])
+    arrive(z_in, z_s.at[0])
+    arrive(slices.at[:, pl.ds(0, 7)], t_s.at[0])
+    to_other.wait_send()
+    arrive(chips.at[pl.ds(0, 15)], last_s.at[1])
 
 
 def write_kernel(mesons_v, traces_v, mesons_h, traces_h, sem):
@@ -359,15 +354,14 @@
             pltpu.VMEM((CHUNKS, 8, 8, 128), f32),
             pltpu.VMEM((8, 8, 128), f32),
             pltpu.VMEM((8, 8, 128), f32),
-            pltpu.VMEM((4, 4, 128), f32),
-            pltpu.VMEM((8, 4, 128), f32),
+            pltpu.VMEM((2, 4, 128), f32),
+            pltpu.VMEM((16, 4, 128), f32),
             dma((2,)), dma((4,)), dma((4,)),
-            dma((CHUNKS,)), dma((CHUNKS,)),
-            dma((CHUNKS,)), dma((CHUNKS,)),
-            dma((CHUNKS, 7)), dma((CHUNKS, 7)),
-            dma((CHUNKS, 7)), dma((CHUNKS, 7)),
-            dma((3,)), dma((3,)),
-            dma((7,)), dma((7,)),
+            dma((1,)), dma((CHUNKS,)),
+            dma((1,)), dma((CHUNKS,)),
+            dma((1,)), dma((CHUNKS,)),
+            dma((1,)), dma((CHUNKS,)),
+            dma((2,)), dma((2,)),
         ],
         compiler_params=pltpu.CompilerParams(
             collective_id=0, has_side_effects=True, vmem_limit_bytes=66700000

time: 40.2 us -> 37 us (0.920)
  Pallas kernels: 39.5 us -> 36.3 us
    pallas_call x1, Pallas kernels: 38.9 us -> 35.7 us  [local(): pl.pallas_call(fields_kernel, out_shape=(pltpu.VMEM((2, 4 * CHUNKS, 2, 64...]
where the time goes in v5:
time: 37 us; the launch traced here: 36.9 us
  Pallas kernels  36.3 us (98%)
  between operations  0.64 us (2%)
    pallas_call x1, Pallas kernels, local(): pl.pallas_call(fields_kernel, out_shape=(pltpu.VMEM((2, 4 * CHUNKS, 2, 64...  35.7 us

profile of v5, /device:TPU:1, one launch (start us, length us, event | category | flops | bytes accessed | tf_op | source)
XLA Modules:
  0.0 36.9 jit_solution(17279524174227874747)
XLA Ops:
  0.6 35.7 %meson_fields.1 = (f32[2,28,2,64]{3,2,1,0:T(2,128)S(1)}, f32[8,2,27]{2,1,0:T(2,128)S(1)}) custom-call(s32[3,27]{1,0:T(4,128)} %bitcast.9, s32[2,8]{1,0:T(2,128)} %bitcast.10, s32[12,64,512]{2,1,0:T(8,128)} %bitcast.7, bf16[12,512,128]{2,1,0:T(8,128)(2,1)} %bitcast.8), custom_call_target="tpu_custom_call" | custom-call | tf_op jit(solution)/shard_map/meson_fields/pallas_call | solution.py:331
  36.3 0.6 %write_out.1 = (f32[2,27,2,64]{3,2,1,0:T(2,128)}, f32[8,2,27]{2,1,0:T(2,128)}) custom-call(f32[2,28,2,64]{3,2,1,0:T(2,128)S(1)} %get-tuple-element.6.mesons_v, f32[8,2,27]{2,1,0:T(2,128)S(1)} %get-tuple-element.7.traces_v), custom_call_target="tpu_custom_call" | custom-call | tf_op jit(solution)/shard_map/write_out/pallas_call | solution.py:371

commit v6 on v5

--- a/solution.py
+++ b/solution.py
@@ -12,6 +12,7 @@
 CHUNKS = 7
 SIZE1, SIZE2 = 1.625, 1.1325
 MESH = pl.DeviceIdType.MESH
+OTHERS = [(e, d) for e in range(2) for d in range(8) if (e, d) != (0, 0)]
 
 
 def iota(shape, dim):
@@ -33,7 +34,7 @@
 def fields_kernel(
     mom_h, pair_h, noise_h, vec_h, mesons, traces,
     mom_s, pair_s, spread, noise_v, vec_v, hrow, kap_r, kap_i,
-    raw, core_in, half, y_in, own, z_in, slices, here, turned, both, chips,
+    raw, core_in, half, y_in, own, z_in, slices, here, turned, chips,
     small_sem, noise_sem, vec_sem, core_s, core_r, y_s, y_r, z_s, z_r, t_s, t_r, last_s, last_r,
 ):
     space, tm = lax.axis_index("space"), lax.axis_index("tm")
@@ -49,8 +50,8 @@
     def in_chips(e, d):
         return {"space": (lax.rem(z + d, 8) * 4 + quad) ^ (2 * e), "tm": tm}
 
-    def in_tm(d):
-        return {"space": space, "tm": lax.rem(tm + d, 8)}
+    def in_tm(e, d):
+        return {"space": space ^ e, "tm": lax.rem(tm + d, 8)}
 
     def load(tile):
         lanes = pl.ds(tile * 128, 128)
@@ -74,7 +75,7 @@
         pl.semaphore_signal(barrier, inc=1, device_id=in_quad(d), device_id_type=MESH)
     for d in range(1, 8):
         pl.semaphore_signal(barrier, inc=1, device_id=in_z(d), device_id_type=MESH)
-        pl.semaphore_signal(barrier, inc=1, device_id=in_tm(d), device_id_type=MESH)
+        pl.semaphore_signal(barrier, inc=1, device_id=in_tm(0, d), device_id_type=MESH)
 
     for k in range(5):
         hrow[k, 0] = jnp.zeros((64, 128), jnp.float32)
@@ -178,10 +179,12 @@
             send_sem=z_s.at[0], recv_sem=z_r.at[g], device_id=in_z(d), device_id_type=MESH,
         )
 
-    def to_tm(g, d):
-        return pltpu.make_async_remote_copy(
-            src_ref=slices.at[g, tm], dst_ref=slices.at[g, tm],
-            send_sem=t_s.at[0], recv_sem=t_r.at[g], device_id=in_tm(d), device_id_type=MESH,
+    mine = core * 8 + tm
+
+    def to_tm(g, e, d):
+        return pltpu.make_async_remote_copy(
+            src_ref=slices.at[g, mine], dst_ref=slices.at[g, mine],
+            send_sem=t_s.at[0], recv_sem=t_r.at[g], device_id=in_tm(e, d), device_id_type=MESH,
         )
 
     def arrive(ref, sem):
@@ -251,9 +254,9 @@
         for k in range(4):
             for c in range(2):
                 mesons[c, 4 * g + k] = total[2 * k : 2 * k + 2, 64 * c : 64 * c + 64]
-        slices[g, tm] = total
-        for d in range(1, 8):
-            to_tm(g, d).start()
+        slices[g, mine] = total
+        for e, d in OTHERS:
+            to_tm(g, e, d).start()
         return 0
 
     lax.fori_loop(0, CHUNKS, after_z, 0)
@@ -261,41 +264,34 @@
     lanes = iota((8, 128), 1)
 
     def after_tm(g, sums):
-        arrive(slices.at[g, pl.ds(0, 7)], t_r.at[g])
-        for t in range(8):
-            tile = slices[g, t]
-            here[t] = tile
-            turned[t] = swap_halves(jnp.where(lanes < 64, tile, -tile))
+        arrive(slices.at[g, pl.ds(0, 15)], t_r.at[g])
+        for c in range(2):
+            for t in range(8):
+                tile = slices[g, 8 * c + t]
+                here[t, c] = tile
+                turned[t, c] = swap_halves(jnp.where(lanes < 64, tile, -tile))
         for k in range(8):
             sink, source, rotated = here[pair_s[1, k]], here[pair_s[0, k]], turned[pair_s[0, k]]
             for c, term in enumerate((sink * source, sink * rotated)):
-                value = jnp.sum(term, axis=1, keepdims=True)
+                value = jnp.sum(term[0] + term[1], axis=1, keepdims=True)
                 sums = jnp.where(lanes == 16 * g + 2 * k + c, value, sums)
         return sums
 
     result = lax.fori_loop(0, CHUNKS, after_tm, jnp.zeros((8, 128), jnp.float32))
     result = result + pltpu.roll(result, 7, 0)
+    chip = z * 2 + y
+
+    def to_chip(e, d):
+        return pltpu.make_async_remote_copy(
+            src_ref=chips.at[chip], dst_ref=chips.at[chip], send_sem=last_s.at[0], recv_sem=last_r.at[0],
+            device_id=in_chips(e, d), device_id_type=MESH,
+        )
+
     for k in range(4):
-        both[core, k : k + 1, :] = result[2 * k : 2 * k + 1, :]
-    to_other = pltpu.make_async_remote_copy(
-        src_ref=both.at[core], dst_ref=both.at[core], send_sem=last_s.at[0], recv_sem=last_r.at[0],
-        device_id=in_quad(1), device_id_type=MESH,
-    )
-    chip = z * 2 + y
-
-    def to_chip(e, d):
-        return pltpu.make_async_remote_copy(
-            src_ref=chips.at[chip], dst_ref=chips.at[chip], send_sem=last_s.at[1], recv_sem=last_r.at[1],
-            device_id=in_chips(e, d), device_id_type=MESH,
-        )
-
-    to_other.start()
-    to_other.wait_recv()
-    chips[chip] = both[0] + both[1]
-    for e in range(2):
-        for d in range(1 - e, 8):
-            to_chip(e, d).start()
-    arrive(chips.at[pl.ds(0, 15)], last_r.at[1])
+        chips[chip, k : k + 1, :] = result[2 * k : 2 * k + 1, :]
+    for e, d in OTHERS:
+        to_chip(e, d).start()
+    arrive(chips.at[pl.ds(0, 15)], last_r.at[0])
     total = chips[0]
     for k in range(1, 16):
         total += chips[k]
@@ -307,9 +303,8 @@
     arrive(raw.at[0], core_s.at[0])
     arrive(y_in, y_s.at[0])
     arrive(z_in, z_s.at[0])
-    arrive(slices.at[:, pl.ds(0, 7)], t_s.at[0])
-    to_other.wait_send()
-    arrive(chips.at[pl.ds(0, 15)], last_s.at[1])
+    arrive(slices.at[:, pl.ds(0, 15)], t_s.at[0])
+    arrive(chips.at[pl.ds(0, 15)], last_s.at[0])
 
 
 def write_kernel(mesons_v, traces_v, mesons_h, traces_h, sem):
@@ -351,17 +346,16 @@
             pltpu.VMEM((CHUNKS, 4, 16, 128), f32),
             pltpu.VMEM((CHUNKS, 8, 8, 128), f32),
             pltpu.VMEM((CHUNKS, 7, 8, 128), f32),
-            pltpu.VMEM((CHUNKS, 8, 8, 128), f32),
-            pltpu.VMEM((8, 8, 128), f32),
-            pltpu.VMEM((8, 8, 128), f32),
-            pltpu.VMEM((2, 4, 128), f32),
+            pltpu.VMEM((CHUNKS, 16, 8, 128), f32),
+            pltpu.VMEM((8, 2, 8, 128), f32),
+            pltpu.VMEM((8, 2, 8, 128), f32),
             pltpu.VMEM((16, 4, 128), f32),
             dma((2,)), dma((4,)), dma((4,)),
             dma((1,)), dma((CHUNKS,)),
             dma((1,)), dma((CHUNKS,)),
             dma((1,)), dma((CHUNKS,)),
             dma((1,)), dma((CHUNKS,)),
-            dma((2,)), dma((2,)),
+            dma((1,)), dma((1,)),
         ],
         compiler_params=pltpu.CompilerParams(
             collective_id=0, has_side_effects=True, vmem_limit_bytes=66700000

time: 37 us -> 36.2 us (0.978)
  Pallas kernels: 36.3 us -> 35.5 us
    pallas_call x1, Pallas kernels: 35.7 us -> 34.8 us  [local(): pl.pallas_call(fields_kernel, out_shape=(pltpu.VMEM((2, 4 * CHUNKS, 2, 64...]
where the time goes in v6:
time: 36.2 us; the launch traced here: 36.1 us
  Pallas kernels  35.5 us (98%)
  between operations  0.64 us (2%)
    pallas_call x1, Pallas kernels, local(): pl.pallas_call(fields_kernel, out_shape=(pltpu.VMEM((2, 4 * CHUNKS, 2, 64...  34.8 us

profile of v6, /device:TPU:1, one launch (start us, length us, event | category | flops | bytes accessed | tf_op | source)
XLA Modules:
  0.0 36.1 jit_solution(9574774885582673945)
XLA Ops:
  0.6 34.8 %meson_fields.1 = (f32[2,28,2,64]{3,2,1,0:T(2,128)S(1)}, f32[8,2,27]{2,1,0:T(2,128)S(1)}) custom-call(s32[3,27]{1,0:T(4,128)} %bitcast.9, s32[2,8]{1,0:T(2,128)} %bitcast.10, s32[12,64,512]{2,1,0:T(8,128)} %bitcast.7, bf16[12,512,128]{2,1,0:T(8,128)(2,1)} %bitcast.8), custom_call_target="tpu_custom_call" | custom-call | tf_op jit(solution)/shard_map/meson_fields/pallas_call | solution.py:326
  35.5 0.6 %write_out.1 = (f32[2,27,2,64]{3,2,1,0:T(2,128)}, f32[8,2,27]{2,1,0:T(2,128)}) custom-call(f32[2,28,2,64]{3,2,1,0:T(2,128)S(1)} %get-tuple-element.6.mesons_v, f32[8,2,27]{2,1,0:T(2,128)S(1)} %get-tuple-element.7.traces_v), custom_call_target="tpu_custom_call" | custom-call | tf_op jit(solution)/shard_map/write_out/pallas_call | solution.py:365

commit v7 on v6

--- a/solution.py
+++ b/solution.py
@@ -10,9 +10,11 @@
 EXTENT = 48
 MOMS = 27
 CHUNKS = 7
+LAG = 1
 SIZE1, SIZE2 = 1.625, 1.1325
 MESH = pl.DeviceIdType.MESH
-OTHERS = [(e, d) for e in range(2) for d in range(8) if (e, d) != (0, 0)]
+FAR_FIRST = (4, 3, 5, 2, 6, 1, 7)
+OTHERS = [(e, d) for d in FAR_FIRST for e in (1, 0)] + [(1, 0)]
 
 
 def iota(shape, dim):
@@ -60,6 +62,13 @@
             pltpu.make_async_copy(vec_h.at[:, lanes, :], vec_v.at[tile], vec_sem.at[tile]),
         )
 
+    barrier = pltpu.get_barrier_semaphore()
+    for d in FAR_FIRST:
+        pl.semaphore_signal(barrier, inc=1, device_id=in_z(d), device_id_type=MESH)
+        pl.semaphore_signal(barrier, inc=1, device_id=in_tm(0, d), device_id_type=MESH)
+    for d in range(1, 3):
+        pl.semaphore_signal(barrier, inc=1, device_id=in_quad(d), device_id_type=MESH)
+
     small = (
         pltpu.make_async_copy(mom_h, mom_s, small_sem.at[0]),
         pltpu.make_async_copy(pair_h, pair_s, small_sem.at[1]),
@@ -69,13 +78,6 @@
     for tile in range(4):
         for copy in load(tile):
             copy.start()
-
-    barrier = pltpu.get_barrier_semaphore()
-    for d in range(1, 3):
-        pl.semaphore_signal(barrier, inc=1, device_id=in_quad(d), device_id_type=MESH)
-    for d in range(1, 8):
-        pl.semaphore_signal(barrier, inc=1, device_id=in_z(d), device_id_type=MESH)
-        pl.semaphore_signal(barrier, inc=1, device_id=in_tm(0, d), device_id_type=MESH)
 
     for k in range(5):
         hrow[k, 0] = jnp.zeros((64, 128), jnp.float32)
@@ -221,14 +223,15 @@
             momentum(g, k)
         to_core(g).start()
 
-        @pl.when(g >= 1)
+        @pl.when(g >= LAG)
         def _():
-            after_core(g - 1)
+            after_core(g - LAG)
 
         return 0
 
     lax.fori_loop(0, CHUNKS, first_step, 0)
-    after_core(CHUNKS - 1)
+    for g in range(CHUNKS - LAG, CHUNKS):
+        after_core(g)
 
     def after_y(g, _):
         to_y(g).wait_recv()
@@ -240,7 +243,7 @@
                 pair = swapped(low[0][bit], low[1][bit], 4)
                 for upper in range(2):
                     own[g, 4 * top + 2 * upper + bit] = pair[upper]
-        for d in range(1, 8):
+        for d in FAR_FIRST:
             to_z(g, d).start()
         return 0
 

time: 36.2 us -> 36 us (level)
  no operation moved by 1% of the time
where the time goes in v7:
time: 36 us; the launch traced here: 35.9 us
  Pallas kernels  35.3 us (98%)
  between operations  0.64 us (2%)
    pallas_call x1, Pallas kernels, local(): pl.pallas_call(fields_kernel, out_shape=(pltpu.VMEM((2, 4 * CHUNKS, 2, 64...  34.6 us

profile of v7, /device:TPU:1, one launch (start us, length us, event | category | flops | bytes accessed | tf_op | source)
XLA Modules:
  0.0 35.9 jit_solution(14399707373582808299)
XLA Ops:
  0.6 34.6 %meson_fields.1 = (f32[2,28,2,64]{3,2,1,0:T(2,128)S(1)}, f32[8,2,27]{2,1,0:T(2,128)S(1)}) custom-call(s32[3,27]{1,0:T(4,128)} %bitcast.9, s32[2,8]{1,0:T(2,128)} %bitcast.10, s32[12,64,512]{2,1,0:T(8,128)} %bitcast.7, bf16[12,512,128]{2,1,0:T(8,128)(2,1)} %bitcast.8), custom_call_target="tpu_custom_call" | custom-call | tf_op jit(solution)/shard_map/meson_fields/pallas_call | solution.py:329
  35.2 0.6 %write_out.1 = (f32[2,27,2,64]{3,2,1,0:T(2,128)}, f32[8,2,27]{2,1,0:T(2,128)}) custom-call(f32[2,28,2,64]{3,2,1,0:T(2,128)S(1)} %get-tuple-element.6.mesons_v, f32[8,2,27]{2,1,0:T(2,128)S(1)} %get-tuple-element.7.traces_v), custom_call_target="tpu_custom_call" | custom-call | tf_op jit(solution)/shard_map/write_out/pallas_call | solution.py:368

commit v8 on v7

--- a/solution.py
+++ b/solution.py
@@ -62,13 +62,6 @@
             pltpu.make_async_copy(vec_h.at[:, lanes, :], vec_v.at[tile], vec_sem.at[tile]),
         )
 
-    barrier = pltpu.get_barrier_semaphore()
-    for d in FAR_FIRST:
-        pl.semaphore_signal(barrier, inc=1, device_id=in_z(d), device_id_type=MESH)
-        pl.semaphore_signal(barrier, inc=1, device_id=in_tm(0, d), device_id_type=MESH)
-    for d in range(1, 3):
-        pl.semaphore_signal(barrier, inc=1, device_id=in_quad(d), device_id_type=MESH)
-
     small = (
         pltpu.make_async_copy(mom_h, mom_s, small_sem.at[0]),
         pltpu.make_async_copy(pair_h, pair_s, small_sem.at[1]),
@@ -78,6 +71,13 @@
     for tile in range(4):
         for copy in load(tile):
             copy.start()
+
+    barrier = pltpu.get_barrier_semaphore()
+    for d in FAR_FIRST:
+        pl.semaphore_signal(barrier, inc=1, device_id=in_z(d), device_id_type=MESH)
+        pl.semaphore_signal(barrier, inc=1, device_id=in_tm(0, d), device_id_type=MESH)
+    for d in range(1, 3):
+        pl.semaphore_signal(barrier, inc=1, device_id=in_quad(d), device_id_type=MESH)
 
     for k in range(5):
         hrow[k, 0] = jnp.zeros((64, 128), jnp.float32)
@@ -161,7 +161,6 @@
         return 0
 
     lax.fori_loop(0, 4, tile_step, 0)
-    pl.semaphore_wait(barrier, 16)
 
     def to_core(g):
         return pltpu.make_async_remote_copy(
@@ -221,6 +220,10 @@
     def first_step(g, _):
         for k in range(4):
             momentum(g, k)
+        @pl.when(g == 0)
+        def _():
+            pl.semaphore_wait(barrier, 16)
+
         to_core(g).start()
 
         @pl.when(g >= LAG)

time: 36 us -> 35.8 us (level)
  no operation moved by 1% of the time
where the time goes in v8:
time: 35.8 us; the launch traced here: 35.7 us
  Pallas kernels  35.1 us (98%)
  between operations  0.64 us (2%)
    pallas_call x1, Pallas kernels, local(): pl.pallas_call(fields_kernel, out_shape=(pltpu.VMEM((2, 4 * CHUNKS, 2, 64...  34.5 us

profile of v8, /device:TPU:1, one launch (start us, length us, event | category | flops | bytes accessed | tf_op | source)
XLA Modules:
  0.0 35.7 jit_solution(15068153357851518509)
XLA Ops:
  0.6 34.5 %meson_fields.1 = (f32[2,28,2,64]{3,2,1,0:T(2,128)S(1)}, f32[8,2,27]{2,1,0:T(2,128)S(1)}) custom-call(s32[3,27]{1,0:T(4,128)} %bitcast.9, s32[2,8]{1,0:T(2,128)} %bitcast.10, s32[12,64,512]{2,1,0:T(8,128)} %bitcast.7, bf16[12,512,128]{2,1,0:T(8,128)(2,1)} %bitcast.8), custom_call_target="tpu_custom_call" | custom-call | tf_op jit(solution)/shard_map/meson_fields/pallas_call | solution.py:332
  35.1 0.6 %write_out.1 = (f32[2,27,2,64]{3,2,1,0:T(2,128)}, f32[8,2,27]{2,1,0:T(2,128)}) custom-call(f32[2,28,2,64]{3,2,1,0:T(2,128)S(1)} %get-tuple-element.6.mesons_v, f32[8,2,27]{2,1,0:T(2,128)S(1)} %get-tuple-element.7.traces_v), custom_call_target="tpu_custom_call" | custom-call | tf_op jit(solution)/shard_map/write_out/pallas_call | solution.py:371
